TPU v7x, 128 devices: a whole 4x4x4 slice. The times are simulated.
128 devices in a mesh: dp: 1, sp: 16 (over z, y), tp: 8 (over x, core).
Axes of the slice: x: 4, y: 4, z: 4, core: 2. Of those that a mesh axis runs over, the one named last changes fastest.
Arguments:
- latents: bfloat16 [3, 256, 1280], P('dp')
- queries: bfloat16 [3, 4096, 768], P('dp', 'sp')
- lat_ln1: float32 [1280], replicated
- lat_wq: bfloat16 [1280, 8, 160], P(None, 'tp')
- lat_wk: bfloat16 [1280, 8, 160], P(None, 'tp')
- lat_wv: bfloat16 [1280, 8, 160], P(None, 'tp')
- lat_wo: bfloat16 [8, 160, 1280], P('tp')
- lat_ln2: float32 [1280], replicated
- lat_up: bfloat16 [1280, 1280], P(None, 'tp')
- lat_down: bfloat16 [1280, 1280], P('tp')
- dec_lnq: float32 [768], replicated
- dec_lnkv: float32 [1280], replicated
- dec_wq: bfloat16 [768, 768], replicated
- dec_wk: bfloat16 [1280, 768], replicated
- dec_wv: bfloat16 [1280, 768], replicated
- dec_wo: bfloat16 [768, 768], replicated
- dec_ln: float32 [768], replicated
- dec_up: bfloat16 [768, 768], replicated
- dec_down: bfloat16 [768, 768], replicated
- dec_out: bfloat16 [768, 32000], replicated
Outputs:
- output: bfloat16 [3, 4096, 32000], P('dp', 'sp')
All inputs are finite; a program needn't handle non-finite values.
Results may differ from a plain program's by a relative error of at most 0.02.
Values are sent between devices in bfloat16 or wider.
A program may use at most 1 GiB of HBM per device.

v0:
```python
import jax
import jax.numpy as jnp
from jax import lax
from jax.sharding import PartitionSpec as P

LN_EPS = 1e-5


def layer_norm(rows_in, gain_vec):
    widened = rows_in.astype(jnp.float32)
    row_mean = jnp.mean(widened, axis=-1, keepdims=True)
    row_var = jnp.mean(jnp.square(widened - row_mean), axis=-1, keepdims=True)
    return ((widened - row_mean) * lax.rsqrt(row_var + LN_EPS) * gain_vec).astype(jnp.bfloat16)


def decode_rows(query_rows, all_keys, all_values, dec_lnq, dec_wq, dec_wo, dec_ln, dec_up, dec_down, dec_out):
    q_proj = jnp.dot(layer_norm(query_rows, dec_lnq), dec_wq, preferred_element_type=jnp.float32).astype(jnp.bfloat16)
    scores = jnp.einsum("crd,cld->crl", q_proj, all_keys, preferred_element_type=jnp.float32) * dec_wq.shape[1] ** -0.5
    attn_probs = jax.nn.softmax(scores, axis=-1).astype(jnp.bfloat16)
    context = jnp.einsum("crl,cld->crd", attn_probs, all_values, preferred_element_type=jnp.float32).astype(jnp.bfloat16)
    mixed_rows = (q_proj.astype(jnp.float32) + jnp.dot(context, dec_wo, preferred_element_type=jnp.float32)).astype(jnp.bfloat16)
    hidden = jax.nn.gelu(jnp.dot(layer_norm(mixed_rows, dec_ln), dec_up, preferred_element_type=jnp.float32), approximate=False).astype(jnp.bfloat16)
    final_rows = (mixed_rows.astype(jnp.float32) + jnp.dot(hidden, dec_down, preferred_element_type=jnp.float32)).astype(jnp.bfloat16)
    return jnp.dot(final_rows, dec_out, preferred_element_type=jnp.float32).astype(jnp.bfloat16)


def solution(mesh):
    tp_size = mesh.shape["tp"]
    head_split = P(None, "tp", None)
    whole_vec = P(None)
    whole_mat = P(None, None)
    in_specs = (P("dp", None, None), P("dp", "sp", None), whole_vec, head_split, head_split, head_split, P("tp", None, None), whole_vec, P(None, "tp"), P("tp", None), whole_vec, whole_vec, whole_mat, whole_mat, whole_mat, whole_mat, whole_vec, whole_mat, whole_mat, whole_mat)

    def local_step(latents, queries, lat_ln1, lat_wq, lat_wk, lat_wv, lat_wo, lat_ln2, lat_up, lat_down, dec_lnq, dec_lnkv, dec_wq, dec_wk, dec_wv, dec_wo, dec_ln, dec_up, dec_down, dec_out):
        tp_index = lax.axis_index("tp")
        head_dim = lat_wq.shape[2]
        normed = layer_norm(latents, lat_ln1)
        q_heads = jnp.einsum("bnd,dhe->bnhe", normed, lat_wq, preferred_element_type=jnp.float32).astype(jnp.bfloat16)
        k_heads = jnp.einsum("bnd,dhe->bnhe", normed, lat_wk, preferred_element_type=jnp.float32).astype(jnp.bfloat16)
        v_heads = jnp.einsum("bnd,dhe->bnhe", normed, lat_wv, preferred_element_type=jnp.float32).astype(jnp.bfloat16)
        scores = jnp.einsum("bqhe,bkhe->bhqk", q_heads, k_heads, preferred_element_type=jnp.float32) * head_dim ** -0.5
        attn_probs = jax.nn.softmax(scores, axis=-1).astype(jnp.bfloat16)
        context = jnp.einsum("bhqk,bkhe->bqhe", attn_probs, v_heads, preferred_element_type=jnp.float32).astype(jnp.bfloat16)
        attn_part = jnp.einsum("crif,ife->cre", context, lat_wo, preferred_element_type=jnp.float32).astype(jnp.bfloat16)
        attn_sum = lax.psum(attn_part, "tp")
        z_mid = (latents.astype(jnp.float32) + attn_sum.astype(jnp.float32)).astype(jnp.bfloat16)
        hidden = jax.nn.gelu(jnp.dot(layer_norm(z_mid, lat_ln2), lat_up, preferred_element_type=jnp.float32), approximate=False).astype(jnp.bfloat16)
        mlp_part = jnp.dot(hidden, lat_down, preferred_element_type=jnp.float32).astype(jnp.bfloat16)
        mlp_rows = lax.psum_scatter(mlp_part, "tp", scatter_dimension=1, tiled=True)
        row_count = mlp_rows.shape[1]
        mid_rows = lax.dynamic_slice_in_dim(z_mid, tp_index * row_count, row_count, axis=1)
        new_rows = (mid_rows.astype(jnp.float32) + mlp_rows.astype(jnp.float32)).astype(jnp.bfloat16)
        kv_in = layer_norm(new_rows, dec_lnkv)
        key_rows = jnp.dot(kv_in, dec_wk, preferred_element_type=jnp.float32).astype(jnp.bfloat16)
        value_rows = jnp.dot(kv_in, dec_wv, preferred_element_type=jnp.float32).astype(jnp.bfloat16)
        all_keys = lax.all_gather(key_rows, "tp", axis=1, tiled=True)
        all_values = lax.all_gather(value_rows, "tp", axis=1, tiled=True)
        query_count = queries.shape[1] // tp_size
        query_rows = lax.dynamic_slice_in_dim(queries, tp_index * query_count, query_count, axis=1)
        out_rows = decode_rows(query_rows, all_keys, all_values, dec_lnq, dec_wq, dec_wo, dec_ln, dec_up, dec_down, dec_out)
        return lax.all_gather(out_rows, "tp", axis=1, tiled=True)

    return jax.shard_map(local_step, mesh=mesh, in_specs=in_specs, out_specs=P("dp", "sp", None), check_vma=False)
```

profile of v0, /device:TPU:1, one launch (start us, length us, event | category | flops | bytes accessed | tf_op | source)
XLA Modules:
  0.0 466.1 jit_solution(161843004611090881)
XLA Ops:
  6.5 0.0 copy-start
  6.6 2.0 convert_reduce_fusion
  8.6 0.2 copy-done.2
  8.8 0.7 fusion.11
  9.5 0.0 copy-start.12
  9.5 1.0 convolution_convert_fusion.3
  10.5 0.0 copy-done.12
  10.5 2.8 convolution_multiply_fusion
  13.3 0.2 fusion.324
  13.5 2.9 fusion.43
  16.4 0.0 copy-done.7
  16.4 2.0 convolution_convert_fusion.1
  18.4 0.0 all-reduce.2.cloned.1.call-update
  18.4 0.0 reduce-scatter.2.cloned.1.call-start
  18.5 66.5 %all-reduce.2.cloned.1.call-done = bf16[3,256,1280]{2,1,0:T(8,128)(2,1)} async-done(((bf16[3,256,1280]{2,1,0:T(8,128)(2,1)}), bf16[3,256,1280]{2,1,0:T(8,128)(2,1)}) %all-reduce.2.cloned.1.call-update) | async-done | bytes 1966096 | tf_op jit(solution)/shard_map/psum | solution.py:45
  84.9 2.8 convert_reduce_fusion.1
  87.7 0.0 copy-start.13
  87.7 0.0 copy-start.16
  87.7 0.7 fusion.14
  88.4 0.6 copy-done.13
  89.0 0.0 copy-done.16
  89.0 1.1 fusion.214
  90.1 3.0 convolution_convert_fusion
  93.1 0.0 reduce-scatter.2.cloned.1.call-update
  93.2 0.0 all-gather.4.cloned.1.call-start
  93.2 32.4 %reduce-scatter.2.cloned.1.call-done = bf16[3,32,1280]{2,1,0:T(8,128)(2,1)} async-done(((bf16[3,256,1280]{2,1,0:T(8,128)(2,1)}), bf16[3,32,1280]{2,1,0:T(8,128)(2,1)}) %reduce-scatter.2.cloned.1.call-update) | async-done | bytes 245776 | tf_op jit(solution)/shard_map/reduce_scatter | solution.py:49
  125.6 1.2 convert_reduce_fusion.2
  126.8 0.2 fusion.73
  127.1 1.2 fusion.47
  128.2 0.0 all-gather.4.cloned.1.call-update
  128.3 0.0 all-gather.6.cloned.1.call-start
  128.3 2.8 fusion.50
  131.1 0.0 all-gather.6.cloned.1.call-update
  131.1 0.2 all-gather.8.cloned.1.call-start
  131.4 1.1 convert_reduce_fusion.3
  132.5 1.1 fusion.96
  133.6 1.3 fusion.44
  134.9 18.8 %all-gather.4.cloned.1.call-done = bf16[3,256,768]{2,1,0:T(8,128)(2,1)} async-done(((bf16[3,32,768]{2,1,0:T(8,128)(2,1)}), bf16[3,256,768]{2,1,0:T(8,128)(2,1)}) %all-gather.4.cloned.1.call-update) | async-done | bytes 1179664 | tf_op jit(solution)/shard_map/all_gather | solution.py:56
  153.7 1.7 convolution_multiply_fusion.1
  155.4 0.2 fusion.325
  155.6 23.0 %all-gather.6.cloned.1.call-done = bf16[3,256,768]{2,1,0:T(8,128)(2,1)} async-done(((bf16[3,32,768]{2,1,0:T(8,128)(2,1)}), bf16[3,256,768]{2,1,0:T(8,128)(2,1)}) %all-gather.6.cloned.1.call-update) | async-done | bytes 1179664 | tf_op jit(solution)/shard_map/all_gather | solution.py:57
  178.6 2.0 fusion.326
  180.6 0.2 multiply_reduce_fusion
  180.8 0.4 fusion.217
  181.2 22.0 %fusion.4 = bf16[3,32,32000]{2,1,0:T(8,128)(2,1)} fusion(bf16[768,32000]{1,0:T(8,128)(2,1)} %param.39, f32[3,32,768]{2,1,0:T(8,128)S(1)} %get-tuple-element.15, bf16[768,768]{1,0:T(8,128)(2,1)} %param.38, f32[3,32,768]{2,1,0:T(8,128)S(1)} %get-tuple-element.16, u8[32,768]{1,0:T(8,128)(4,1)S(1)} %get-tuple-element.8, u8[32,768]{1,0:T(8,128)(4,1)S(1)} %get-tuple-element.7), kind=kOutput, calls=%fused_computation.4 | convolution fusion | flops 4840218624 | bytes 57114624 | tf_op jit(solution)/shard_map/dot_general | solution.py:24
  203.2 0.0 all-gather.8.cloned.1.call-update
  203.2 223.1 %all-gather.8.cloned.1.call-done = bf16[3,256,32000]{2,1,0:T(8,128)(2,1)} async-done(((bf16[3,32,32000]{2,1,0:T(8,128)(2,1)}), bf16[3,256,32000]{2,1,0:T(8,128)(2,1)}) %all-gather.8.cloned.1.call-update) | async-done | bytes 49152016 | tf_op jit(solution)/shard_map/all_gather | solution.py:61
  426.4 33.2 %copy.25 = bf16[3,256,32000]{2,1,0:T(8,128)(2,1)} copy(bf16[3,256,32000]{2,1,0:T(8,128)(2,1)} %all-gather.8.cloned.1.call-done) | data formatting | bytes 98304000
  (36 shorter events, 0.1 us)
Async XLA Ops:
  6.5 120.5 %copy-start = (bf16[1280,768]{1,0:T(8,128)(2,1)S(1)}, bf16[1280,768]{1,0:T(8,128)(2,1)}, u32[]{:S(2)}) copy-start(bf16[1280,768]{1,0:T(8,128)(2,1)} %param.33) | copy-start | bytes 5898244
  6.5 3.0 copy-start.15
  6.5 78.4 %all-reduce.2.cloned.1.call-start = ((), (), s32[]{:S(2)}) async-start(), calls=%async_computation.1 | async-start | bytes 3932160 | tf_op jit(solution)/shard_map/psum | solution.py:45
  6.5 2.3 copy-start.2
  6.5 3.0 copy-start.11
  9.5 1.0 copy-start.12
  13.5 2.9 copy-start.7
  18.4 107.2 %reduce-scatter.2.cloned.1.call-start = ((), (), s32[]{:S(2)}) async-start(), calls=%async_computation.2 | async-start | bytes 2211840 | tf_op jit(solution)/shard_map/reduce_scatter | solution.py:49
  87.7 2.4 copy-start.3
  87.7 1.3 copy-start.13
  87.7 1.3 copy-start.16
  89.0 1.1 copy-start.14
  93.1 33.9 %copy-start.8 = (f32[1280]{0:T(1024)S(1)}, f32[1280]{0:T(1024)}, u32[]{:S(2)}) copy-start(f32[1280]{0:T(1024)} %param.31) | copy-start | bytes 15364
  93.2 60.5 %all-gather.4.cloned.1.call-start = ((), (), s32[]{:S(2)}) async-start(), calls=%async_computation.3 | async-start | bytes 1327104 | tf_op jit(solution)/shard_map/all_gather | solution.py:56
  128.2 5.4 %copy-start.6 = (bf16[768,768]{1,0:T(8,128)(2,1)S(1)}, bf16[768,768]{1,0:T(8,128)(2,1)}, u32[]{:S(2)}) copy-start(bf16[768,768]{1,0:T(8,128)(2,1)} %param.32) | copy-start | bytes 3538948
  128.2 5.4 %copy-start.9 = (f32[768]{0:T(1024)S(1)}, f32[768]{0:T(1024)}, u32[]{:S(2)}) copy-start(f32[768]{0:T(1024)} %param.30) | copy-start | bytes 9220
  128.3 50.3 %all-gather.6.cloned.1.call-start = ((), (), s32[]{:S(2)}) async-start(), calls=%async_computation.4 | async-start | bytes 1327104 | tf_op jit(solution)/shard_map/all_gather | solution.py:57
  131.1 47.5 %copy-start.4 = (bf16[768,768]{1,0:T(8,128)(2,1)S(1)}, bf16[768,768]{1,0:T(8,128)(2,1)}, u32[]{:S(2)}) copy-start(bf16[768,768]{1,0:T(8,128)(2,1)} %param.35) | copy-start | bytes 3538948
  131.1 295.2 %all-gather.8.cloned.1.call-start = ((), (), s32[]{:S(2)}) async-start(), calls=%async_computation.5 | async-start | bytes 55296000 | tf_op jit(solution)/shard_map/all_gather | solution.py:61
  155.4 25.4 %copy-start.5 = (bf16[768,768]{1,0:T(8,128)(2,1)S(1)}, bf16[768,768]{1,0:T(8,128)(2,1)}, u32[]{:S(2)}) copy-start(bf16[768,768]{1,0:T(8,128)(2,1)} %param.37) | copy-start | bytes 3538948
  155.4 25.4 %copy-start.10 = (f32[768]{0:T(1024)S(1)}, f32[768]{0:T(1024)}, u32[]{:S(2)}) copy-start(f32[768]{0:T(1024)} %param.36) | copy-start | bytes 9220
  426.4 33.2 %copy-start.1 = (bf16[1280,768]{1,0:T(8,128)(2,1)S(1)}, bf16[1280,768]{1,0:T(8,128)(2,1)}, u32[]{:S(2)}) copy-start(bf16[1280,768]{1,0:T(8,128)(2,1)} %param.33) | copy-start | bytes 5898244
Sparse Core Ops, SparseCore 0:
  18.5 66.3 all-reduce.1
  93.3 32.2 reduce-scatter.1
  128.4 25.2 all-gather.3
  155.2 23.3 all-gather.5
  203.3 222.9 all-gather.7
where the time goes:
time: 466 us
  waiting for transfers between devices  364 us (78%)
  matrix products  44.1 us (9%)
  local copies, waits for them, and re-layouts  34.1 us (7%)
  between operations  13.4 us (3%)
  other arithmetic  10.4 us (2%)
    all_gather x1, waiting for transfers between devices, local_step(): return lax.all_gather(out_rows, 'tp', axis=1, tiled=True)  223 us
    psum x1, waiting for transfers between devices, local_step(): attn_sum = lax.psum(attn_part, 'tp')  66.5 us
    unnamed x35, local copies, waits for them, and re-layouts  34.1 us
    reduce_scatter x1, waiting for transfers between devices, local_step(): mlp_rows = lax.psum_scatter(mlp_part, 'tp', scatter_dimension=1, tiled=True)  32.4 us
    all_gather x1, waiting for transfers between devices, local_step(): all_values = lax.all_gather(value_rows, 'tp', axis=1, tiled=True)  23 us
    dot_general x1, matrix products, decode_rows(): jnp.dot(final_rows, dec_out, preferred_element_type=jnp.float32)  22 us
    all_gather x1, waiting for transfers between devices, local_step(): all_keys = lax.all_gather(key_rows, 'tp', axis=1, tiled=True)  18.8 us
  transfers between devices with their start and end apart: 5, of which 5 were waited for; matrix products, arithmetic and copies ran while one was open for 2% of the time, Pallas kernels for 0%

commit v1 on v0

--- a/solution.py
+++ b/solution.py
@@ -25,7 +25,6 @@
 
 
 def solution(mesh):
-    tp_size = mesh.shape["tp"]
     head_split = P(None, "tp", None)
     whole_vec = P(None)
     whole_mat = P(None, None)
@@ -55,9 +54,6 @@
         value_rows = jnp.dot(kv_in, dec_wv, preferred_element_type=jnp.float32).astype(jnp.bfloat16)
         all_keys = lax.all_gather(key_rows, "tp", axis=1, tiled=True)
         all_values = lax.all_gather(value_rows, "tp", axis=1, tiled=True)
-        query_count = queries.shape[1] // tp_size
-        query_rows = lax.dynamic_slice_in_dim(queries, tp_index * query_count, query_count, axis=1)
-        out_rows = decode_rows(query_rows, all_keys, all_values, dec_lnq, dec_wq, dec_wo, dec_ln, dec_up, dec_down, dec_out)
-        return lax.all_gather(out_rows, "tp", axis=1, tiled=True)
+        return decode_rows(queries, all_keys, all_values, dec_lnq, dec_wq, dec_wo, dec_ln, dec_up, dec_down, dec_out)
 
     return jax.shard_map(local_step, mesh=mesh, in_specs=in_specs, out_specs=P("dp", "sp", None), check_vma=False)

time: 466 us -> 246 us (0.53)
  waiting for transfers between devices: 364 us -> 141 us
  matrix products: 44.1 us -> 81.7 us
  local copies, waits for them, and re-layouts: 34.1 us -> 0.3 us
    all_gather x1 -> x0, waiting for transfers between devices: 223 us -> none  [local_step(): return lax.all_gather(out_rows, 'tp', axis=1, tiled=True)]
    unnamed x35 -> x32, local copies, waits for them, and re-layouts: 34.1 us -> 0.3 us
    dot_general x1, matrix products: 22 us -> 47.1 us  [decode_rows(): jnp.dot(final_rows, dec_out, preferred_element_type=jnp.float32)]
    dot_general x0 -> x1, matrix products: none -> 7.49 us  [decode_rows(): jnp.dot(hidden, dec_down, preferred_element_type=jnp.float32)]
  transfers between devices with their start and end apart: 5 -> 4, of which waited for: 5 -> 4; matrix products, arithmetic and copies ran while one was open for 2% -> 3% of each run, Pallas kernels for 0% -> 0%
where the time goes in v1:
time: 246 us
  waiting for transfers between devices  141 us (57%)
  matrix products  81.7 us (33%)
  between operations  13.4 us (5%)
  other arithmetic  9.18 us (4%)
    psum x1, waiting for transfers between devices, local_step(): attn_sum = lax.psum(attn_part, 'tp')  66.4 us
    dot_general x1, matrix products, decode_rows(): jnp.dot(final_rows, dec_out, preferred_element_type=jnp.float32)  47.1 us
    reduce_scatter x1, waiting for transfers between devices, local_step(): mlp_rows = lax.psum_scatter(mlp_part, 'tp', scatter_dimension=1, tiled=True)  32.4 us
    all_gather x1, waiting for transfers between devices, local_step(): all_values = lax.all_gather(value_rows, 'tp', axis=1, tiled=True)  22.9 us
    all_gather x1, waiting for transfers between devices, local_step(): all_keys = lax.all_gather(key_rows, 'tp', axis=1, tiled=True)  19.2 us
    dot_general x1, matrix products, decode_rows(): jnp.dot(hidden, dec_down, preferred_element_type=jnp.float32)  7.49 us
    reduce_sum x4, other arithmetic, layer_norm(): row_mean = jnp.mean(widened, axis=-1, keepdims=True)  6.25 us
  transfers between devices with their start and end apart: 4, of which 4 were waited for; matrix products, arithmetic and copies ran while one was open for 3% of the time, Pallas kernels for 0%

profile of v1, /device:TPU:1, one launch (start us, length us, event | category | flops | bytes accessed | tf_op | source)
XLA Modules:
  0.0 246.0 jit_solution(15970578985722828649)
XLA Ops:
  6.6 2.0 convert_reduce_fusion
  8.6 0.2 copy-done.2
  8.8 0.7 fusion.7
  9.5 0.0 copy-done.12
  9.5 0.0 copy-done.8
  9.5 0.0 copy-start.9
  9.5 1.0 convolution_convert_fusion.6
  10.5 0.0 copy-done.9
  10.5 2.8 %convolution_multiply_fusion.1 = f32[3,256,256]{1,2,0:T(8,128)S(1)} fusion(bf16[3,256,160]{1,2,0:T(8,128)(2,1)S(1)} %convolution_convert_fusion.6, bf16[3,256,1280]{2,1,0:T(8,128)(2,1)} %param.20, f32[1280]{0:T(1024)S(1)} %copy-done.12, f32[3,256]{1,0:T(4,128)S(1)} %add_rsqrt_fusion.2, f32[3,256]{1,0:T(4,128)S(1)} %broadcast_multiply_fusion.1, ...), kind=kOutput, calls=%fused_computation.76 | convolution fusion | flops 382722048 | bytes 3419136 | tf_op jit(solution)/shard_map/bqhe,bkhe->bhqk/dot_general | solution.py:40
  13.3 0.2 fusion.236
  13.5 2.9 %fusion.91 = bf16[3,256,160]{1,2,0:T(8,128)(2,1)S(1)} fusion(bf16[3,256,1280]{2,1,0:T(8,128)(2,1)} %param.20, f32[1280]{0:T(1024)S(1)} %copy-done.12, f32[3,256]{1,0:T(4,128)S(1)} %add_rsqrt_fusion.2, f32[3,256]{1,0:T(4,128)S(1)} %broadcast_multiply_fusion.1, bf16[1280,1,160]{0,2,1:T(8,128)(2,1)} %param.25, f32[3,256]{1,0:T(4,128)S(1)} %fusion.236, ...), kind=kOutput, calls=%fused_computation.122 | convolution fusion | flops 383239168 | bytes 3422208 | tf_op jit(solution)/shard_map/bhqk,bkhe->bqhe/dot_general | solution.py:42
  16.4 2.0 convolution_convert_fusion.2
  18.4 0.0 all-reduce.2.cloned.1.call-update
  18.4 0.0 copy-start.10
  18.4 0.0 copy-start.13
  18.4 0.0 reduce-scatter.2.cloned.1.call-start
  18.5 66.4 %all-reduce.2.cloned.1.call-done = bf16[3,256,1280]{2,1,0:T(8,128)(2,1)} async-done(((bf16[3,256,1280]{2,1,0:T(8,128)(2,1)}), bf16[3,256,1280]{2,1,0:T(8,128)(2,1)}) %all-reduce.2.cloned.1.call-update) | async-done | bytes 1966096 | tf_op jit(solution)/shard_map/psum | solution.py:44
  84.9 2.8 %convert_reduce_fusion.1 = (f32[3,256]{1,0:T(4,128)S(1)}, bf16[3,256,1280]{2,1,0:T(8,128)(2,1)S(1)}) fusion(bf16[3,256,1280]{2,1,0:T(8,128)(2,1)} %all-reduce.2.cloned.1.call-done, bf16[3,256,1280]{2,1,0:T(8,128)(2,1)} %param.20), kind=kLoop, calls=%fused_computation.8 | loop fusion | flops 5897472 | bytes 5901312 | tf_op jit(solution)/shard_map/reduce_sum | solution.py:11
  87.7 0.7 fusion.10
  88.4 0.0 copy-start.11
  88.4 1.0 fusion.167
  89.5 0.0 copy-done.3
  89.5 3.0 %convolution_convert_fusion.1 = bf16[3,256,1280]{2,1,0:T(8,128)(2,1)} fusion(bf16[160,1280]{1,0:T(8,128)(2,1)S(1)} %copy-done.11, f32[3,256,160]{1,2,0:T(8,128)S(1)} %get-tuple-element.13, u8[256,160]{0,1:T(8,128)(4,1)S(1)} %get-tuple-element.8, u8[256,160]{0,1:T(8,128)(4,1)S(1)} %get-tuple-element.7), kind=kOutput, calls=%fused_computation.24 | convolution fusion | flops 324157440 | bytes 2949120 | tf_op jit(solution)/shard_map/dot_general | solution.py:47
  92.5 0.0 reduce-scatter.2.cloned.1.call-update
  92.5 0.0 all-gather.3.cloned.1.call-start
  92.6 32.4 %reduce-scatter.2.cloned.1.call-done = bf16[3,32,1280]{2,1,0:T(8,128)(2,1)} async-done(((bf16[3,256,1280]{2,1,0:T(8,128)(2,1)}), bf16[3,32,1280]{2,1,0:T(8,128)(2,1)}) %reduce-scatter.2.cloned.1.call-update) | async-done | bytes 245776 | tf_op jit(solution)/shard_map/reduce_scatter | solution.py:48
  125.0 1.2 convert_reduce_fusion.4
  126.2 0.2 fusion.107
  126.5 0.0 copy-start.4
  126.5 1.2 fusion.92
  127.6 0.0 all-gather.3.cloned.1.call-update
  127.7 0.0 copy-start.14
  127.7 0.2 all-gather.5.cloned.1.call-start
  127.9 2.7 %fusion.95 = bf16[3,32,768]{2,1,0:T(8,128)(2,1)} fusion(bf16[1280,768]{1,0:T(8,128)(2,1)} %param.34, bf16[3,32,1280]{2,1,0:T(8,128)(2,1)S(1)} %get-tuple-element.10, f32[1280]{0:T(1024)S(1)} %copy-done.6, f32[3,32]{1,0:T(4,128)S(1)} %add_rsqrt_fusion.4, f32[3,32]{1,0:T(4,128)S(1)} %broadcast_multiply_fusion.4), kind=kOutput, calls=%fused_computation.124 | convolution fusion | flops 189431808 | bytes 2365184 | tf_op jit(solution)/shard_map/dot_general | solution.py:54
  130.6 0.0 all-gather.5.cloned.1.call-update
  130.7 0.2 convert_reduce_fusion.3
  130.9 0.5 fusion.21
  131.4 2.5 convolution_convert_fusion.4
  133.8 19.2 %all-gather.3.cloned.1.call-done = bf16[3,256,768]{2,1,0:T(8,128)(2,1)} async-done(((bf16[3,32,768]{2,1,0:T(8,128)(2,1)}), bf16[3,256,768]{2,1,0:T(8,128)(2,1)}) %all-gather.3.cloned.1.call-update) | async-done | bytes 1179664 | tf_op jit(solution)/shard_map/all_gather | solution.py:55
  153.1 1.8 convolution_multiply_fusion
  154.9 0.2 fusion.237
  155.1 22.9 %all-gather.5.cloned.1.call-done = bf16[3,256,768]{2,1,0:T(8,128)(2,1)} async-done(((bf16[3,32,768]{2,1,0:T(8,128)(2,1)}), bf16[3,256,768]{2,1,0:T(8,128)(2,1)}) %all-gather.5.cloned.1.call-update) | async-done | bytes 1179664 | tf_op jit(solution)/shard_map/all_gather | solution.py:56
  178.0 3.2 %convert_reduce_fusion.2 = (f32[3,256]{1,0:T(4,128)S(1)}, bf16[3,256,768]{2,1,0:T(8,128)(2,1)S(1)}) fusion(bf16[768,768]{1,0:T(8,128)(2,1)} %param.35, bf16[3,256,768]{2,1,0:T(8,128)(2,1)} %all-gather.5.cloned.1.call-done, f32[3,256]{1,0:T(4,128)S(1)} %fusion.237, f32[3,256,256]{1,2,0:T(8,128)S(1)} %convolution_multiply_fusion, ...), kind=kOutput, calls=%fused_computation.23 | convolution fusion | flops 1212088576 | bytes 5511168 | tf_op jit(solution)/shard_map/dot_general | solution.py:21
  181.2 0.5 fusion.18
  181.7 0.0 copy-start.7
  181.7 3.1 %fusion.99 = (u8[256,768]{1,0:T(8,128)(4,1)S(1)}, u8[256,768]{1,0:T(8,128)(4,1)S(1)}, f32[3,256,768]{2,1,0:T(8,128)S(1)}) fusion(bf16[768,768]{1,0:T(8,128)(2,1)} %param.37, bf16[3,256,768]{2,1,0:T(8,128)(2,1)S(1)} %get-tuple-element.15, f32[768]{0:T(1024)S(1)} %copy-done.15, f32[3,256]{1,0:T(4,128)S(1)} %add_rsqrt_fusion, ...), kind=kOutput, calls=%fused_computation.131 | convolution fusion | flops 916193280 | bytes 5121024 | tf_op jit(solution)/shard_map/dot_general | solution.py:22
  184.9 7.5 %fusion.24 = bf16[3,256,768]{2,1,0:T(8,128)(2,1)} fusion(bf16[3,256,768]{2,1,0:T(8,128)(2,1)S(1)} %get-tuple-element.15, f32[3,256,768]{2,1,0:T(8,128)S(1)} %get-tuple-element.16, bf16[768,768]{1,0:T(8,128)(2,1)S(1)} %copy-done.7, u8[256,768]{1,0:T(8,128)(4,1)S(1)} %get-tuple-element.6, u8[256,768]{1,0:T(8,128)(4,1)S(1)} %get-tuple-element.5), kind=kOutput, calls=%fused_computation.38 | convolution fusion | flops 949026816 | bytes 6291456 | tf_op jit(solution)/shard_map/dot_general | solution.py:23
  192.3 47.1 %convolution_convert_fusion = bf16[3,256,32000]{2,1,0:T(8,128)(2,1)} fusion(bf16[3,256,768]{2,1,0:T(8,128)(2,1)} %fusion.24, bf16[768,32000]{1,0:T(8,128)(2,1)} %param.39), kind=kOutput, calls=%fused_computation.2 | convolution fusion | flops 37773312000 | bytes 99483648 | tf_op jit(solution)/shard_map/dot_general | solution.py:24
  (31 shorter events, 0.1 us)
Async XLA Ops:
  6.5 119.9 %copy-start = (bf16[1280,768]{1,0:T(8,128)(2,1)S(1)}, bf16[1280,768]{1,0:T(8,128)(2,1)}, u32[]{:S(2)}) copy-start(bf16[1280,768]{1,0:T(8,128)(2,1)} %param.33) | copy-start | bytes 5898244
  6.5 3.0 %copy-start.12 = (f32[1280]{0:T(1024)S(1)}, f32[1280]{0:T(1024)}, u32[]{:S(2)}) copy-start(f32[1280]{0:T(1024)} %param.22) | copy-start | bytes 15364
  6.5 78.4 %all-reduce.2.cloned.1.call-start = ((), (), s32[]{:S(2)}) async-start(), calls=%async_computation.1 | async-start | bytes 3932160 | tf_op jit(solution)/shard_map/psum | solution.py:44
  6.5 2.3 copy-start.2
  6.5 3.0 %copy-start.8 = (bf16[1280,1,160]{0,2,1:T(8,128)(2,1)S(1)}, bf16[1280,1,160]{0,2,1:T(8,128)(2,1)}, u32[]{:S(2)}) copy-start(bf16[1280,1,160]{0,2,1:T(8,128)(2,1)} %param.24) | copy-start | bytes 1228804
  9.5 1.0 copy-start.9
  13.5 2.9 %copy-start.5 = (bf16[1,160,1280]{2,1,0:T(8,128)(2,1)S(1)}, bf16[1,160,1280]{2,1,0:T(8,128)(2,1)}, u32[]{:S(2)}) copy-start(bf16[1,160,1280]{2,1,0:T(8,128)(2,1)} %param.26) | copy-start | bytes 1228804
  18.4 70.0 %copy-start.10 = (bf16[1280,160]{0,1:T(8,128)(2,1)S(1)}, bf16[1280,160]{0,1:T(8,128)(2,1)}, u32[]{:S(2)}) copy-start(bf16[1280,160]{0,1:T(8,128)(2,1)} %param.28) | copy-start | bytes 1228804
  18.4 70.0 %copy-start.13 = (f32[1280]{0:T(1024)S(1)}, f32[1280]{0:T(1024)}, u32[]{:S(2)}) copy-start(f32[1280]{0:T(1024)} %param.27) | copy-start | bytes 15364
  18.4 106.6 %reduce-scatter.2.cloned.1.call-start = ((), (), s32[]{:S(2)}) async-start(), calls=%async_computation.2 | async-start | bytes 2211840 | tf_op jit(solution)/shard_map/reduce_scatter | solution.py:48
  87.7 1.8 copy-start.3
  88.4 1.1 copy-start.11
  92.5 33.9 %copy-start.6 = (f32[1280]{0:T(1024)S(1)}, f32[1280]{0:T(1024)}, u32[]{:S(2)}) copy-start(f32[1280]{0:T(1024)} %param.31) | copy-start | bytes 15364
  92.5 60.5 %all-gather.3.cloned.1.call-start = ((), (), s32[]{:S(2)}) async-start(), calls=%async_computation.3 | async-start | bytes 1327104 | tf_op jit(solution)/shard_map/all_gather | solution.py:55
  126.5 4.2 %copy-start.4 = (bf16[3,256,768]{2,1,0:T(8,128)(2,1)S(1)}, bf16[3,256,768]{2,1,0:T(8,128)(2,1)}, u32[]{:S(2)}) copy-start(bf16[3,256,768]{2,1,0:T(8,128)(2,1)} %param.21) | copy-start | bytes 3538948
  127.7 3.7 %copy-start.14 = (f32[768]{0:T(1024)S(1)}, f32[768]{0:T(1024)}, u32[]{:S(2)}) copy-start(f32[768]{0:T(1024)} %param.30) | copy-start | bytes 9220
  127.7 50.3 %all-gather.5.cloned.1.call-start = ((), (), s32[]{:S(2)}) async-start(), calls=%async_computation.4 | async-start | bytes 1327104 | tf_op jit(solution)/shard_map/all_gather | solution.py:56
  155.1 26.6 %copy-start.15 = (f32[768]{0:T(1024)S(1)}, f32[768]{0:T(1024)}, u32[]{:S(2)}) copy-start(f32[768]{0:T(1024)} %param.36) | copy-start | bytes 9220
  181.7 3.2 %copy-start.7 = (bf16[768,768]{1,0:T(8,128)(2,1)S(1)}, bf16[768,768]{1,0:T(8,128)(2,1)}, u32[]{:S(2)}) copy-start(bf16[768,768]{1,0:T(8,128)(2,1)} %param.38) | copy-start | bytes 3538948
  192.3 47.1 %copy-start.1 = (bf16[1280,768]{1,0:T(8,128)(2,1)S(1)}, bf16[1280,768]{1,0:T(8,128)(2,1)}, u32[]{:S(2)}) copy-start(bf16[1280,768]{1,0:T(8,128)(2,1)} %param.33) | copy-start | bytes 5898244
Sparse Core Ops, SparseCore 0:
  18.5 66.3 all-reduce.1
  92.7 32.2 reduce-scatter.1
  127.8 25.2 all-gather.2
  154.6 23.3 all-gather.4

commit v2 on v1

v2 whole, which is shorter than its diff:
```python
import functools

import jax
import jax.numpy as jnp
from jax import lax
from jax.experimental import pallas as pl
from jax.experimental.pallas import tpu as pltpu
from jax.sharding import PartitionSpec as P

LN_EPS = 1e-5
MESH = pl.DeviceIdType.MESH
F32 = jnp.float32
BF16 = jnp.bfloat16


def norm_rows(widened, gain_row):
    row_mean = jnp.mean(widened, axis=-1, keepdims=True)
    centred = widened - row_mean
    row_var = jnp.mean(jnp.square(centred), axis=-1, keepdims=True)
    return (centred * lax.rsqrt(row_var + LN_EPS) * gain_row).astype(BF16)


def gelu(val):
    return 0.5 * val * (1.0 + lax.erf(val * (0.5**0.5)))


def dot(lhs, rhs):
    return jnp.dot(lhs, rhs, preferred_element_type=F32)


def dot_t(lhs, rhs):
    return lax.dot_general(lhs, rhs, (((1,), (1,)), ((), ())), preferred_element_type=F32)


def softmax(scores):
    shifted = jnp.exp(scores - jnp.max(scores, axis=-1, keepdims=True))
    return (shifted / jnp.sum(shifted, axis=-1, keepdims=True)).astype(BF16)


def front_kernel(
    z_hbm, q_hbm, wq_hbm, wk_hbm, wv_hbm, wo_hbm, up_hbm, down_hbm, dwq_hbm, dwk_hbm, dwv_hbm, dwo_hbm, dup_hbm, ddn_hbm,
    g1, g2, gq, gkv, gd,
    x2_hbm,
    z, zr, wqkv, wrest, queries, dwq, dwk, dwv, dwo, dup, ddn,
    normed, khead, vhead, part1, part2, kbuf, vbuf, qd, x2,
    load_sem, out_sem, pair_sem, x_sem, k1_sem, v1_sem, k2_sem, v2_sem, k3_sem, v3_sem,
):
    sp, tp = lax.axis_index("sp"), lax.axis_index("tp")
    zc, yc = sp // 4, sp % 4
    xc, core = tp // 2, tp % 2
    items, latents, width = z.shape
    rows = items * 8

    partner = {"tp": tp + 1 - 2 * core}
    x_peer = [{"tp": ((xc + d) % 4) * 2 + core} for d in (1, 2, 3)]
    y_peer = [{"sp": zc * 4 + (yc + d) % 4} for d in (1, 2, 3)]
    z_peer = [{"sp": ((zc + d) % 4) * 4 + yc} for d in (1, 2, 3)]

    def remote(src, dst, sems, where):
        copy = pltpu.make_async_remote_copy(
            src_ref=src, dst_ref=dst, send_sem=sems.at[0], recv_sem=sems.at[1], device_id=where, device_id_type=MESH)
        copy.start()
        return copy

    barrier = pltpu.get_barrier_semaphore()
    peers = [partner] + x_peer + y_peer + z_peer
    for peer in peers:
        pl.semaphore_signal(barrier, inc=1, device_id=peer, device_id_type=MESH)

    loads = []

    def load(src, dst):
        copy = pltpu.make_async_copy(src, dst, load_sem.at[len(loads)])
        copy.start()
        loads.append(copy)
        return copy

    load_q = [load(src, wqkv.at[0, i]) for i, src in enumerate((wq_hbm, wk_hbm, wv_hbm))]
    load_z = load(z_hbm, z)
    load_zr = load(z_hbm.at[:, pl.ds(pl.multiple_of(sp * 16 + core * 8, 8), 8), :], zr)
    load_r = [load(src, wrest.at[0, i]) for i, src in enumerate((wo_hbm, up_hbm, down_hbm))]
    load_dq = [load(q_hbm, queries), load(dwq_hbm, dwq)]
    load_kv = [load(dwk_hbm, dwk), load(dwv_hbm, dwv)]
    load_dec = [load(dwo_hbm, dwo), load(dup_hbm, dup), load(ddn_hbm, ddn)]

    for copy in load_q:
        copy.wait()
    pl.semaphore_wait(barrier, len(peers))
    swap_q = remote(wqkv.at[0], wqkv.at[1], pair_sem.at[0], partner)
    for copy in load_r:
        copy.wait()
    swap_r = remote(wrest.at[0], wrest.at[1], pair_sem.at[1], partner)

    load_z.wait()
    for b in range(items):
        def norm_step(i, carry, b=b):
            at = pl.multiple_of(i * 32, 32)
            normed[pl.ds(pl.multiple_of(b * latents + at, 32), 32), :] = norm_rows(z[b, pl.ds(at, 32), :].astype(F32), g1[...])
            return carry
        lax.fori_loop(0, latents // 32, norm_step, 0)
    load_zr.wait()
    z_rows = zr[...].astype(F32).reshape(rows, width)
    normed_rows = norm_rows(z_rows, g1[...])

    attn = jnp.zeros((rows, width), F32)
    for h in range(2):
        if h == 1:
            swap_q.wait_recv()
        q_rows = dot_t(normed_rows, wqkv[h, 0]).astype(BF16)
        khead[...] = dot_t(normed[...], wqkv[h, 1]).astype(BF16)
        vhead[...] = dot_t(normed[...], wqkv[h, 2]).astype(BF16)
        wide = dot_t(q_rows, khead[...])
        scores = jnp.concatenate([wide[8 * b : 8 * b + 8, latents * b : latents * (b + 1)] for b in range(items)], axis=0)
        probs = softmax(scores * q_rows.shape[1] ** -0.5)
        context = jnp.concatenate(
            [dot(probs, vhead[latents * b : latents * (b + 1), :])[8 * b : 8 * b + 8] for b in range(items)], axis=0).astype(BF16)
        if h == 1:
            swap_r.wait_recv()
        attn = attn + dot(context, wrest[h, 0])
    part1[xc] = attn.astype(BF16)
    sent1 = [remote(part1.at[xc], part1.at[xc], x_sem.at[0, d], x_peer[d]) for d in range(3)]

    for copy in load_dq:
        copy.wait()
    for b in range(items):
        at = latents * b
        qd[at : at + latents, :] = dot(norm_rows(queries[b].astype(F32), gq[...]), dwq[...]).astype(BF16)

    for copy in sent1:
        copy.wait_recv()
    total = part1[0].astype(F32)
    for s in range(1, 4):
        total = total + part1[s].astype(F32)
    z_mid = (z_rows + total).astype(BF16)
    normed_mid = norm_rows(z_mid.astype(F32), g2[...])
    mlp = jnp.zeros((rows, width), F32)
    for h in range(2):
        hidden = gelu(dot_t(normed_mid, wrest[h, 1])).astype(BF16)
        mlp = mlp + dot(hidden, wrest[h, 2])
    part2[xc] = mlp.astype(BF16)
    sent2 = [remote(part2.at[xc], part2.at[xc], x_sem.at[1, d], x_peer[d]) for d in range(3)]

    for copy in load_kv:
        copy.wait()
    for copy in sent2:
        copy.wait_recv()
    total = part2[0].astype(F32)
    for s in range(1, 4):
        total = total + part2[s].astype(F32)
    z_new = (z_mid.astype(F32) + total).astype(BF16)
    kv_in = norm_rows(z_new.astype(F32), gkv[...])
    for b_, (buf, wt) in enumerate(((kbuf, dwk), (vbuf, dwv))):
        val = dot(kv_in, wt[...])
        for b in range(items):
            buf[b, core, zc, yc] = val[8 * b : 8 * b + 8].astype(BF16)

    k1 = [[remote(kbuf.at[b, core, zc, yc], kbuf.at[b, core, zc, yc], k1_sem.at[b, d], y_peer[d]) for d in range(3)] for b in range(items)]
    v1 = [[remote(vbuf.at[b, core, zc, yc], vbuf.at[b, core, zc, yc], v1_sem.at[b, d], z_peer[d]) for d in range(3)] for b in range(items)]
    for copy in load_dec:
        copy.wait()
    k2, v2, k3, v3 = [], [], [], []
    for b in range(items):
        for copy in k1[b]:
            copy.wait_recv()
        k2.append([remote(kbuf.at[b, core, zc], kbuf.at[b, core, zc], k2_sem.at[b, d], z_peer[d]) for d in range(3)])
        for copy in v1[b]:
            copy.wait_recv()
        v2.append([remote(vbuf.at[b, core, :, yc], vbuf.at[b, core, :, yc], v2_sem.at[b, d], y_peer[d]) for d in range(3)])

    def swap(b):
        for copy in k2[b]:
            copy.wait_recv()
        k3.append(remote(kbuf.at[b, core], kbuf.at[b, core], k3_sem.at[b], partner))
        for copy in v2[b]:
            copy.wait_recv()
        v3.append(remote(vbuf.at[b, core], vbuf.at[b, core], v3_sem.at[b], partner))

    stores = []

    def decode(b):
        at = latents * b
        channels = qd.shape[1]
        q_item = qd[at : at + latents, :]
        k3[b].wait_recv()
        keys = kbuf[b].astype(F32).reshape(latents, channels).astype(BF16)
        probs = softmax(dot_t(q_item, keys) * channels**-0.5)
        v3[b].wait_recv()
        values = vbuf[b].astype(F32).reshape(latents, channels).astype(BF16)
        context = dot(probs, values).astype(BF16)
        mixed = (q_item.astype(F32) + dot(context, dwo[...])).astype(BF16)
        hidden = gelu(dot(norm_rows(mixed.astype(F32), gd[...]), dup[...])).astype(BF16)
        x2[at : at + latents, :] = (mixed.astype(F32) + dot(hidden, ddn[...])).astype(BF16)
        store = pltpu.make_async_copy(x2.at[at : at + latents], x2_hbm.at[at : at + latents], out_sem.at[b])
        store.start()
        stores.append(store)

    swap(0)
    swap(1)
    decode(0)
    swap(2)
    decode(1)
    decode(2)

    for copy in [swap_q, swap_r] + sent1 + sent2 + sum(k1 + v1 + k2 + v2, []) + k3 + v3:
        copy.wait_send()
    for store in stores:
        store.wait()


def front(latents, queries, lat_ws, dec_ws, gains):
    items, lat_rows, width = latents.shape
    channels = queries.shape[2]
    head = lat_ws[0].shape[0]
    anywhere = pl.BlockSpec(memory_space=pl.ANY)
    vmem = pl.BlockSpec(memory_space=pltpu.VMEM)
    total = items * lat_rows
    dma = pltpu.SemaphoreType.DMA
    return pl.pallas_call(
        front_kernel,
        out_shape=jax.ShapeDtypeStruct((total, channels), BF16),
        in_specs=[anywhere] * 14 + [vmem] * 5,
        out_specs=anywhere,
        scratch_shapes=[
            pltpu.VMEM((items, lat_rows, width), BF16),
            pltpu.VMEM((items, 8, width), BF16),
            pltpu.VMEM((2, 3, head, width), BF16),
            pltpu.VMEM((2, 3, head, width), BF16),
            pltpu.VMEM((items, lat_rows, channels), BF16),
            pltpu.VMEM((channels, channels), BF16),
            pltpu.VMEM((width, channels), BF16),
            pltpu.VMEM((width, channels), BF16),
            pltpu.VMEM((channels, channels), BF16),
            pltpu.VMEM((channels, channels), BF16),
            pltpu.VMEM((channels, channels), BF16),
            pltpu.VMEM((total, width), BF16),
            pltpu.VMEM((total, head), BF16),
            pltpu.VMEM((total, head), BF16),
            pltpu.VMEM((4, items * 8, width), BF16),
            pltpu.VMEM((4, items * 8, width), BF16),
            pltpu.VMEM((items, 2, 4, 4, 8, channels), BF16),
            pltpu.VMEM((items, 2, 4, 4, 8, channels), BF16),
            pltpu.VMEM((total, channels), BF16),
            pltpu.VMEM((total, channels), BF16),
            dma((15,)),
            dma((items,)),
            dma((2, 2)),
            dma((2, 3, 2)),
            dma((items, 3, 2)),
            dma((items, 3, 2)),
            dma((items, 3, 2)),
            dma((items, 3, 2)),
            dma((items, 2)),
            dma((items, 2)),
        ],
        compiler_params=pltpu.CompilerParams(collective_id=0, has_side_effects=True, vmem_limit_bytes=48 * 2**20),
        name="front",
    )(latents, queries, *lat_ws, *dec_ws, *gains)


def out_kernel(x2, wt, out):
    for at in range(0, x2.shape[0], 256):
        out[at : at + 256, :] = dot(x2[at : at + 256, :], wt[...]).astype(BF16)


def out_product(x2, dec_out):
    rows, channels = x2.shape
    cols = dec_out.shape[1]
    tile = 3200
    return pl.pallas_call(
        out_kernel,
        grid=(cols // tile,),
        in_specs=[pl.BlockSpec((rows, channels), lambda i: (0, 0)), pl.BlockSpec((channels, tile), lambda i: (0, i))],
        out_specs=pl.BlockSpec((rows, tile), lambda i: (0, i)),
        out_shape=jax.ShapeDtypeStruct((rows, cols), BF16),
        compiler_params=pltpu.CompilerParams(vmem_limit_bytes=56 * 2**20),
        name="out_product",
    )(x2, dec_out)


def solution(mesh):
    head_split = P(None, "tp", None)
    whole_vec = P(None)
    whole_mat = P(None, None)
    in_specs = (P("dp", None, None), P("dp", "sp", None), whole_vec, head_split, head_split, head_split, P("tp", None, None), whole_vec, P(None, "tp"), P("tp", None), whole_vec, whole_vec, whole_mat, whole_mat, whole_mat, whole_mat, whole_vec, whole_mat, whole_mat, whole_mat)

    def local_step(latents, queries, lat_ln1, lat_wq, lat_wk, lat_wv, lat_wo, lat_ln2, lat_up, lat_down, dec_lnq, dec_lnkv, dec_wq, dec_wk, dec_wv, dec_wo, dec_ln, dec_up, dec_down, dec_out):
        lat_ws = [wt[:, 0, :].T for wt in (lat_wq, lat_wk, lat_wv)] + [lat_wo[0], lat_up.T, lat_down]
        gains = [gain[None, :] for gain in (lat_ln1, lat_ln2, dec_lnq, dec_lnkv, dec_ln)]
        x2 = front(latents, queries, lat_ws, [dec_wq, dec_wk, dec_wv, dec_wo, dec_up, dec_down], gains)
        out = out_product(x2, dec_out)
        return out.reshape(queries.shape[0], queries.shape[1], dec_out.shape[1])

    return jax.shard_map(local_step, mesh=mesh, in_specs=in_specs, out_specs=P("dp", "sp", None), check_vma=False)
```

time: 246 us -> 107 us (0.43)
  waiting for transfers between devices: 141 us -> 0 us
  Pallas kernels: 0 us -> 93.3 us
  matrix products: 81.7 us -> 0 us
  between operations: 13.4 us -> 0.03 us
  local copies, waits for them, and re-layouts: 0.3 us -> 13.1 us
  other arithmetic: 9.18 us -> 0 us
    pallas_call x0 -> x2, Pallas kernels: none -> 93.3 us  [the longest x1 46.8 us: out_product(): pl.pallas_call(out_kernel, grid=(cols // tile,), in_specs=[pl.BlockSpec((...]
    dot_general x14 -> x0, matrix products: 81.7 us -> none  [the longest x1 47.1 us: decode_rows(): jnp.dot(final_rows, dec_out, preferred_element_type=jnp.float32)]
    psum x1 -> x0, waiting for transfers between devices: 66.4 us -> none  [local_step(): attn_sum = lax.psum(attn_part, 'tp')]
    all_gather x2 -> x0, waiting for transfers between devices: 42.2 us -> none  [the longest x1 22.9 us: local_step(): all_values = lax.all_gather(value_rows, 'tp', axis=1, tiled=True)]
    reduce_scatter x1 -> x0, waiting for transfers between devices: 32.4 us -> none  [local_step(): mlp_rows = lax.psum_scatter(mlp_part, 'tp', scatter_dimension=1, tiled=True)]
    unnamed x32 -> x18, local copies, waits for them, and re-layouts: 0.3 us -> 9.57 us
    reduce_sum x9 -> x0, other arithmetic: 8.73 us -> none  [the longest x4 6.25 us: layer_norm(): row_mean = jnp.mean(widened, axis=-1, keepdims=True)]
    broadcast_in_dim x0 -> x5, local copies, waits for them, and re-layouts: none -> 3.48 us  [local_step(): gain[None, :]]
  transfers between devices with their start and end apart: 4 -> 0, of which waited for: 4 -> 0; matrix products, arithmetic and copies ran while one was open for 3% -> 0% of each run, Pallas kernels for 0% -> 0%
where the time goes in v2:
time: 107 us; the launch traced here: 106 us
  Pallas kernels  93.3 us (87%)
  local copies, waits for them, and re-layouts  13.1 us (12%)
    pallas_call x1, Pallas kernels, out_product(): pl.pallas_call(out_kernel, grid=(cols // tile,), in_specs=[pl.BlockSpec((...  46.8 us
    pallas_call x1, Pallas kernels, front(): pl.pallas_call(front_kernel, out_shape=jax.ShapeDtypeStruct((total, chann...  46.5 us
    unnamed x18, local copies, waits for them, and re-layouts  9.57 us
    broadcast_in_dim x5, local copies, waits for them, and re-layouts, local_step(): gain[None, :]  3.48 us

profile of v2, /device:TPU:1, one launch (start us, length us, event | category | flops | bytes accessed | tf_op | source)
XLA Modules:
  0.0 106.4 jit_solution(1598652317031813393)
XLA Ops:
  0.0 0.7 broadcast_in_dim.17.gq
  0.7 0.7 broadcast_in_dim.19.gd
  1.4 0.7 broadcast_in_dim.15.g1
  2.1 0.7 broadcast_in_dim.16.g2
  2.8 0.7 broadcast_in_dim.18.gkv
  3.5 0.0 copy-start.1
  3.5 1.3 %copy-done.1 = bf16[3,256,768]{2,1,0:T(8,128)(2,1)S(1)} copy-done((bf16[3,256,768]{2,1,0:T(8,128)(2,1)S(1)}, bf16[3,256,768]{2,1,0:T(8,128)(2,1)}, u32[]{:S(2)}) %copy-start.1) | copy-done | bytes 1179672
  4.8 0.0 copy-start.2
  4.8 1.3 %copy-done.2 = bf16[768,768]{1,0:T(8,128)(2,1)S(1)} copy-done((bf16[768,768]{1,0:T(8,128)(2,1)S(1)}, bf16[768,768]{1,0:T(8,128)(2,1)}, u32[]{:S(2)}) %copy-start.2) | copy-done | bytes 1179672
  6.0 0.0 copy-start.3
  6.0 1.0 copy-done.3
  7.0 0.0 copy-start.4
  7.0 1.0 copy-done.4
  8.0 0.0 copy-start.5
  8.0 1.0 copy-done.5
  9.0 0.0 copy-start.6
  9.0 1.0 copy-done.6
  10.0 0.0 copy-start.7
  10.0 1.0 copy-done.7
  11.0 0.0 copy-start.8
  11.0 1.0 copy-done.8
  12.0 46.5 %front.1.x2 = bf16[768,768]{1,0:T(8,128)(2,1)S(1)} custom-call(bf16[3,256,1280]{2,1,0:T(8,128)(2,1)} %z_hbm.1, bf16[3,256,768]{2,1,0:T(8,128)(2,1)S(1)} %copy-done.1, bf16[160,1280]{1,0:T(8,128)(2,1)S(1)} %bitcast.12, bf16[160,1280]{1,0:T(8,128)(2,1)S(1)} %bitcast.13, bf16[160,1280]{1,0:T(8,128)(2,1)S(1)} %bitcast.14, bf16[160,1280]{1,0:T(8,128)(2,1)S(1)} %bitcast.15, ...), custom_call_target="tpu_custom_call" | custom-call | tf_op jit(solution)/shard_map/front/pallas_call | solution.py:218
  58.5 0.0 copy-start
  58.5 1.0 copy-done
  59.5 46.8 %out_product.1 = bf16[768,32000]{1,0:T(8,128)(2,1)} custom-call(bf16[768,768]{1,0:T(8,128)(2,1)} %copy-done, bf16[768,32000]{1,0:T(8,128)(2,1)} %wt.1), custom_call_target="tpu_custom_call" | custom-call | tf_op jit(solution)/shard_map/out_product/pallas_call | solution.py:269
Async XLA Ops:
  3.5 1.3 %copy-start.1 = (bf16[3,256,768]{2,1,0:T(8,128)(2,1)S(1)}, bf16[3,256,768]{2,1,0:T(8,128)(2,1)}, u32[]{:S(2)}) copy-start(bf16[3,256,768]{2,1,0:T(8,128)(2,1)} %q_hbm.1) | copy-start | bytes 3538948
  4.8 1.3 %copy-start.2 = (bf16[768,768]{1,0:T(8,128)(2,1)S(1)}, bf16[768,768]{1,0:T(8,128)(2,1)}, u32[]{:S(2)}) copy-start(bf16[768,768]{1,0:T(8,128)(2,1)} %dwq_hbm.1) | copy-start | bytes 3538948
  6.0 1.0 copy-start.3
  7.0 1.0 copy-start.4
  8.0 1.0 copy-start.5
  9.0 1.0 copy-start.6
  10.0 1.0 copy-start.7
  11.0 1.0 copy-start.8
  58.5 1.0 copy-start

commit v3 on v2

--- a/solution.py
+++ b/solution.py
@@ -11,6 +11,7 @@
 MESH = pl.DeviceIdType.MESH
 F32 = jnp.float32
 BF16 = jnp.bfloat16
+VMEM_BYTES = 67043328
 
 
 def norm_rows(widened, gain_row):
@@ -39,10 +40,10 @@
 
 def front_kernel(
     z_hbm, q_hbm, wq_hbm, wk_hbm, wv_hbm, wo_hbm, up_hbm, down_hbm, dwq_hbm, dwk_hbm, dwv_hbm, dwo_hbm, dup_hbm, ddn_hbm,
-    g1, g2, gq, gkv, gd,
+    g1_hbm, g2_hbm, gq_hbm, gkv_hbm, gd_hbm,
     x2_hbm,
     z, zr, wqkv, wrest, queries, dwq, dwk, dwv, dwo, dup, ddn,
-    normed, khead, vhead, part1, part2, kbuf, vbuf, qd, x2,
+    g1, g2, gq, gkv, gd, normed, khead, vhead, part1, part2, kbuf, vbuf, qd, x2,
     load_sem, out_sem, pair_sem, x_sem, k1_sem, v1_sem, k2_sem, v2_sem, k3_sem, v3_sem,
 ):
     sp, tp = lax.axis_index("sp"), lax.axis_index("tp")
@@ -75,6 +76,7 @@
         loads.append(copy)
         return copy
 
+    load_g = [load(src, dst) for src, dst in ((g1_hbm, g1), (g2_hbm, g2), (gq_hbm, gq), (gkv_hbm, gkv), (gd_hbm, gd))]
     load_q = [load(src, wqkv.at[0, i]) for i, src in enumerate((wq_hbm, wk_hbm, wv_hbm))]
     load_z = load(z_hbm, z)
     load_zr = load(z_hbm.at[:, pl.ds(pl.multiple_of(sp * 16 + core * 8, 8), 8), :], zr)
@@ -83,7 +85,7 @@
     load_kv = [load(dwk_hbm, dwk), load(dwv_hbm, dwv)]
     load_dec = [load(dwo_hbm, dwo), load(dup_hbm, dup), load(ddn_hbm, ddn)]
 
-    for copy in load_q:
+    for copy in load_g + load_q:
         copy.wait()
     pl.semaphore_wait(barrier, len(peers))
     swap_q = remote(wqkv.at[0], wqkv.at[1], pair_sem.at[0], partner)
@@ -212,13 +214,12 @@
     channels = queries.shape[2]
     head = lat_ws[0].shape[0]
     anywhere = pl.BlockSpec(memory_space=pl.ANY)
-    vmem = pl.BlockSpec(memory_space=pltpu.VMEM)
     total = items * lat_rows
     dma = pltpu.SemaphoreType.DMA
     return pl.pallas_call(
         front_kernel,
         out_shape=jax.ShapeDtypeStruct((total, channels), BF16),
-        in_specs=[anywhere] * 14 + [vmem] * 5,
+        in_specs=[anywhere] * 19,
         out_specs=anywhere,
         scratch_shapes=[
             pltpu.VMEM((items, lat_rows, width), BF16),
@@ -232,6 +233,11 @@
             pltpu.VMEM((channels, channels), BF16),
             pltpu.VMEM((channels, channels), BF16),
             pltpu.VMEM((channels, channels), BF16),
+            pltpu.VMEM((width,), F32),
+            pltpu.VMEM((width,), F32),
+            pltpu.VMEM((channels,), F32),
+            pltpu.VMEM((width,), F32),
+            pltpu.VMEM((channels,), F32),
             pltpu.VMEM((total, width), BF16),
             pltpu.VMEM((total, head), BF16),
             pltpu.VMEM((total, head), BF16),
@@ -241,7 +247,7 @@
             pltpu.VMEM((items, 2, 4, 4, 8, channels), BF16),
             pltpu.VMEM((total, channels), BF16),
             pltpu.VMEM((total, channels), BF16),
-            dma((15,)),
+            dma((20,)),
             dma((items,)),
             dma((2, 2)),
             dma((2, 3, 2)),
@@ -252,27 +258,86 @@
             dma((items, 2)),
             dma((items, 2)),
         ],
-        compiler_params=pltpu.CompilerParams(collective_id=0, has_side_effects=True, vmem_limit_bytes=48 * 2**20),
+        compiler_params=pltpu.CompilerParams(collective_id=0, has_side_effects=True, vmem_limit_bytes=VMEM_BYTES),
         name="front",
     )(latents, queries, *lat_ws, *dec_ws, *gains)
 
 
-def out_kernel(x2, wt, out):
-    for at in range(0, x2.shape[0], 256):
-        out[at : at + 256, :] = dot(x2[at : at + 256, :], wt[...]).astype(BF16)
+def out_kernel(x2_hbm, wt_hbm, out_hbm, x2, wt, out, x2_sem, wt_sem, out_sem):
+    cols = out_hbm.shape[1]
+    slots, _, tile = wt.shape
+    steps, rest = cols // tile, cols % tile
+
+    def fetch(i, slot, size=tile):
+        at = pl.multiple_of(i * tile, tile)
+        return pltpu.make_async_copy(wt_hbm.at[:, pl.ds(at, size)], wt.at[slot, :, :size], wt_sem.at[slot])
+
+    def store(i, slot, size=tile):
+        at = pl.multiple_of(i * tile, tile)
+        return pltpu.make_async_copy(out.at[slot, :, :size], out_hbm.at[:, pl.ds(at, size)], out_sem.at[slot])
+
+    def product(slot, size):
+        for at in range(0, x2.shape[0], 256):
+            out[slot, at : at + 256, :size] = dot(x2[at : at + 256, :], wt[slot, :, :size]).astype(BF16)
+
+    load_x2 = pltpu.make_async_copy(x2_hbm, x2, x2_sem)
+    load_x2.start()
+    for i in range(slots):
+        fetch(i, i).start()
+    load_x2.wait()
+
+    def step(i, carry):
+        slot = i % slots
+        fetch(i, slot).wait()
+
+        @pl.when(i >= slots)
+        def _():
+            store(i - slots, slot).wait()
+
+        product(slot, tile)
+        store(i, slot).start()
+
+        @pl.when(i + slots < steps)
+        def _():
+            fetch(i + slots, slot).start()
+
+        @pl.when(i + slots == steps)
+        def _():
+            fetch(steps, slot, rest).start()
+
+        return carry
+
+    lax.fori_loop(0, steps, step, 0)
+    last = steps % slots
+    fetch(steps, last, rest).wait()
+    store(steps - slots, last).wait()
+    product(last, rest)
+    store(steps, last, rest).start()
+    for i in range(steps - slots + 1, steps):
+        store(i, i % slots).wait()
+    store(steps, last, rest).wait()
 
 
 def out_product(x2, dec_out):
     rows, channels = x2.shape
     cols = dec_out.shape[1]
-    tile = 3200
+    tile, slots = 2048, 3
+    anywhere = pl.BlockSpec(memory_space=pl.ANY)
+    dma = pltpu.SemaphoreType.DMA
     return pl.pallas_call(
         out_kernel,
-        grid=(cols // tile,),
-        in_specs=[pl.BlockSpec((rows, channels), lambda i: (0, 0)), pl.BlockSpec((channels, tile), lambda i: (0, i))],
-        out_specs=pl.BlockSpec((rows, tile), lambda i: (0, i)),
+        in_specs=[anywhere, anywhere],
+        out_specs=anywhere,
         out_shape=jax.ShapeDtypeStruct((rows, cols), BF16),
-        compiler_params=pltpu.CompilerParams(vmem_limit_bytes=56 * 2**20),
+        scratch_shapes=[
+            pltpu.VMEM((rows, channels), BF16),
+            pltpu.VMEM((slots, channels, tile), BF16),
+            pltpu.VMEM((slots, rows, tile), BF16),
+            dma,
+            dma((slots,)),
+            dma((slots,)),
+        ],
+        compiler_params=pltpu.CompilerParams(vmem_limit_bytes=VMEM_BYTES),
         name="out_product",
     )(x2, dec_out)
 
@@ -285,7 +350,7 @@
 
     def local_step(latents, queries, lat_ln1, lat_wq, lat_wk, lat_wv, lat_wo, lat_ln2, lat_up, lat_down, dec_lnq, dec_lnkv, dec_wq, dec_wk, dec_wv, dec_wo, dec_ln, dec_up, dec_down, dec_out):
         lat_ws = [wt[:, 0, :].T for wt in (lat_wq, lat_wk, lat_wv)] + [lat_wo[0], lat_up.T, lat_down]
-        gains = [gain[None, :] for gain in (lat_ln1, lat_ln2, dec_lnq, dec_lnkv, dec_ln)]
+        gains = [lat_ln1, lat_ln2, dec_lnq, dec_lnkv, dec_ln]
         x2 = front(latents, queries, lat_ws, [dec_wq, dec_wk, dec_wv, dec_wo, dec_up, dec_down], gains)
         out = out_product(x2, dec_out)
         return out.reshape(queries.shape[0], queries.shape[1], dec_out.shape[1])

time: 107 us -> 92.2 us (0.86)
  local copies, waits for them, and re-layouts: 13.1 us -> 0 us
  Pallas kernels: 93.3 us -> 92.1 us
    unnamed x18 -> x0, local copies, waits for them, and re-layouts: 9.57 us -> none
    broadcast_in_dim x5 -> x0, local copies, waits for them, and re-layouts: 3.48 us -> none  [local_step(): gain[None, :]]
    pallas_call x1, Pallas kernels: 46.8 us -> 45.5 us  [out_product(): pl.pallas_call(out_kernel, in_specs=[anywhere, anywhere], out_specs=anywh...]
where the time goes in v3:
time: 92.2 us; the launch traced here: 92.1 us
  Pallas kernels  92.1 us (100%)
    pallas_call x1, Pallas kernels, front(): pl.pallas_call(front_kernel, out_shape=jax.ShapeDtypeStruct((total, chann...  46.5 us
    pallas_call x1, Pallas kernels, out_product(): pl.pallas_call(out_kernel, in_specs=[anywhere, anywhere], out_specs=anywh...  45.5 us

profile of v3, /device:TPU:1, one launch (start us, length us, event | category | flops | bytes accessed | tf_op | source)
XLA Modules:
  0.0 92.1 jit_solution(6630904974827658140)
XLA Ops:
  0.0 46.5 %front.1.x2_hbm = bf16[768,768]{1,0:T(8,128)(2,1)} custom-call(bf16[3,256,1280]{2,1,0:T(8,128)(2,1)} %z_hbm.1, bf16[3,256,768]{2,1,0:T(8,128)(2,1)} %q_hbm.1, bf16[160,1280]{1,0:T(8,128)(2,1)} %bitcast.12, bf16[160,1280]{1,0:T(8,128)(2,1)} %bitcast.13, bf16[160,1280]{1,0:T(8,128)(2,1)} %bitcast.14, bf16[160,1280]{1,0:T(8,128)(2,1)} %bitcast.15, ...), custom_call_target="tpu_custom_call" | custom-call | tf_op jit(solution)/shard_map/front/pallas_call | solution.py:219
  46.5 45.5 %out_product.1 = bf16[768,32000]{1,0:T(8,128)(2,1)} custom-call(bf16[768,768]{1,0:T(8,128)(2,1)} %front.1.x2_hbm, bf16[768,32000]{1,0:T(8,128)(2,1)} %wt_hbm.1), custom_call_target="tpu_custom_call" | custom-call | tf_op jit(solution)/shard_map/out_product/pallas_call | solution.py:327

commit v4 on v3

v4 whole, which is shorter than its diff:
```python
import functools

import jax
import jax.numpy as jnp
from jax import lax
from jax.experimental import pallas as pl
from jax.experimental.pallas import tpu as pltpu
from jax.sharding import PartitionSpec as P

LN_EPS = 1e-5
MESH = pl.DeviceIdType.MESH
F32 = jnp.float32
BF16 = jnp.bfloat16
VMEM_BYTES = 67043328


def norm_rows(widened, gain_row):
    row_mean = jnp.mean(widened, axis=-1, keepdims=True)
    centred = widened - row_mean
    row_var = jnp.mean(jnp.square(centred), axis=-1, keepdims=True)
    return (centred * lax.rsqrt(row_var + LN_EPS) * gain_row).astype(BF16)


def gelu(val):
    return 0.5 * val * (1.0 + lax.erf(val * (0.5**0.5)))


def dot(lhs, rhs):
    return jnp.dot(lhs, rhs, preferred_element_type=F32)


def dot_t(lhs, rhs):
    return lax.dot_general(lhs, rhs, (((1,), (1,)), ((), ())), preferred_element_type=F32)


def softmax(scores):
    shifted = jnp.exp(scores - jnp.max(scores, axis=-1, keepdims=True))
    return (shifted / jnp.sum(shifted, axis=-1, keepdims=True)).astype(BF16)


def front_kernel(
    z_hbm, q_hbm, wq_hbm, wk_hbm, wv_hbm, wo_hbm, up_hbm, down_hbm, dwq_hbm, dwk_hbm, dwv_hbm, dwo_hbm, dup_hbm, ddn_hbm,
    g1_hbm, g2_hbm, gq_hbm, gkv_hbm, gd_hbm,
    x2_hbm,
    z, zr, wqkv, wo, wmlp, half, taken, queries, dwq, dwk, dwv, dwo, dup, ddn,
    g1, g2, gq, gkv, gd, normed, khead, vhead, part1, part2, kbuf, vbuf, qd, x2,
    load_sem, out_sem, pair_sem, x_sem, k1_sem, v1_sem, k2_sem, v2_sem, k3_sem, v3_sem, share_sem,
):
    sp, tp = lax.axis_index("sp"), lax.axis_index("tp")
    zc, yc = sp // 4, sp % 4
    xc, core = tp // 2, tp % 2
    items, latents, width = z.shape

    partner = {"tp": tp + 1 - 2 * core}
    x_peer = [{"tp": ((xc + d) % 4) * 2 + core} for d in (1, 2, 3)]
    y_peer = [{"sp": zc * 4 + (yc + d) % 4} for d in (1, 2, 3)]
    z_peer = [{"sp": ((zc + d) % 4) * 4 + yc} for d in (1, 2, 3)]

    def remote(src, dst, sems, where):
        copy = pltpu.make_async_remote_copy(
            src_ref=src, dst_ref=dst, send_sem=sems.at[0], recv_sem=sems.at[1], device_id=where, device_id_type=MESH)
        copy.start()
        return copy

    barrier = pltpu.get_barrier_semaphore()
    peers = [partner] + x_peer + y_peer + z_peer
    for peer in peers:
        pl.semaphore_signal(barrier, inc=1, device_id=peer, device_id_type=MESH)

    loads = []

    def load(src, dst):
        copy = pltpu.make_async_copy(src, dst, load_sem.at[len(loads)])
        copy.start()
        loads.append(copy)
        return copy

    load_g = [load(src, dst) for src, dst in ((g1_hbm, g1), (g2_hbm, g2), (gq_hbm, gq), (gkv_hbm, gkv), (gd_hbm, gd))]
    load_z = [load(z_hbm.at[0], z.at[0])]
    load_q = [load(src, wqkv.at[i]) for i, src in enumerate((wq_hbm, wk_hbm, wv_hbm))]
    load_z += [load(z_hbm.at[b], z.at[b]) for b in range(1, items)]
    load_zr = [load(z_hbm.at[:, pl.ds(pl.multiple_of(sp * 16 + at * 8, 8), 8), :], zr.at[i]) for i, at in enumerate((core, 1 - core))]
    load_r = [load(wo_hbm, wo), load(up_hbm, wmlp.at[0, 0]), load(down_hbm, wmlp.at[0, 1])]
    mine = latents // 2
    load_dq = [load(q_hbm.at[:, pl.ds(pl.multiple_of(core * mine, mine), mine), :], queries), load(dwq_hbm, dwq)]
    load_kv = [load(dwk_hbm, dwk), load(dwv_hbm, dwv)]
    load_dec = [load(dwo_hbm, dwo), load(dup_hbm, dup), load(ddn_hbm, ddn)]

    def norm_item(b):
        for at in range(0, latents, 32):
            normed[b * latents + at : b * latents + at + 32, :] = norm_rows(z[b, at : at + 32, :].astype(F32), g1[...])

    def item(ref, b):
        return ref[latents * b : latents * (b + 1), :]

    def project(b):
        khead[latents * b : latents * (b + 1), :] = dot_t(item(normed, b), wqkv[1]).astype(BF16)
        vhead[latents * b : latents * (b + 1), :] = dot_t(item(normed, b), wqkv[2]).astype(BF16)

    def attend(b):
        chip_rows = jnp.concatenate([zr[0, b].astype(F32), zr[1, b].astype(F32)], axis=0)
        q_rows = dot_t(norm_rows(chip_rows, g1[...]), wqkv[0]).astype(BF16)
        probs = softmax(dot_t(q_rows, item(khead, b)) * q_rows.shape[1] ** -0.5)
        context = dot(probs, item(vhead, b)).astype(BF16)
        return dot(context, wo[...])

    pair, sent1 = [], []

    def give(b, part):
        half[b] = part[8:].astype(BF16)
        pair.append(remote(half.at[b], taken.at[b], pair_sem.at[b], partner))

    def spread(b, part):
        pair[b].wait_recv()
        part1[b, xc] = (part[:8] + taken[b].astype(F32)).astype(BF16)
        sent1.append([remote(part1.at[b, xc], part1.at[b, xc], x_sem.at[0, b, d], x_peer[d]) for d in range(3)])

    for copy in load_g + load_z[:1]:
        copy.wait()
    norm_item(0)
    for copy in load_q + load_z[1:] + load_zr + load_r[:1]:
        copy.wait()
    project(0)
    norm_item(1)
    parts = [attend(0)]
    project(1)
    norm_item(2)
    pl.semaphore_wait(barrier, len(peers))
    give(0, parts[0])
    parts.append(attend(1))
    project(2)
    give(1, parts[1])
    parts.append(attend(2))
    spread(0, parts[0])
    give(2, parts[2])
    for copy in load_r[1:]:
        copy.wait()
    swap_r = remote(wmlp.at[0], wmlp.at[1], pair_sem.at[items], partner)
    spread(1, parts[1])
    spread(2, parts[2])

    for copy in load_dq:
        copy.wait()
    for b in range(items):
        qd[b] = dot(norm_rows(queries[b].astype(F32), gq[...]), dwq[...]).astype(BF16)

    def gather_sum(part, b):
        total = part[b, 0].astype(F32)
        for s in range(1, 4):
            total = total + part[b, s].astype(F32)
        return total

    sent2, z_mid = [], []
    for b in range(items):
        for copy in sent1[b]:
            copy.wait_recv()
        if b == 0:
            swap_r.wait_recv()
        z_mid.append((zr[0, b].astype(F32) + gather_sum(part1, b)).astype(BF16))
        normed_mid = norm_rows(z_mid[b].astype(F32), g2[...])
        mlp = jnp.zeros((8, width), F32)
        for h in range(2):
            hidden = gelu(dot_t(normed_mid, wmlp[h, 0])).astype(BF16)
            mlp = mlp + dot(hidden, wmlp[h, 1])
        part2[b, xc] = mlp.astype(BF16)
        sent2.append([remote(part2.at[b, xc], part2.at[b, xc], x_sem.at[1, b, d], x_peer[d]) for d in range(3)])

    for copy in load_kv:
        copy.wait()
    k1, v1 = [], []
    for b in range(items):
        for copy in sent2[b]:
            copy.wait_recv()
        z_new = (z_mid[b].astype(F32) + gather_sum(part2, b)).astype(BF16)
        kv_in = norm_rows(z_new.astype(F32), gkv[...])
        kbuf[b, core, zc, yc] = dot(kv_in, dwk[...]).astype(BF16)
        vbuf[b, core, zc, yc] = dot(kv_in, dwv[...]).astype(BF16)
        k1.append([remote(kbuf.at[b, core, zc, yc], kbuf.at[b, core, zc, yc], k1_sem.at[b, d], y_peer[d]) for d in range(3)])
        v1.append([remote(vbuf.at[b, core, zc, yc], vbuf.at[b, core, zc, yc], v1_sem.at[b, d], z_peer[d]) for d in range(3)])

    for copy in load_dec:
        copy.wait()
    k2, v2, k3, v3 = [], [], [], []

    def forward_k(b, at, i):
        k3[b].append(remote(kbuf.at[b, core, at], kbuf.at[b, core, at], k3_sem.at[b, i], partner))

    def forward_v(b, at, i):
        v3[b].append(remote(vbuf.at[b, core, :, at], vbuf.at[b, core, :, at], v3_sem.at[b, i], partner))

    for b in range(items):
        k3.append([])
        v3.append([])
        for copy in k1[b]:
            copy.wait_recv()
        k2.append([remote(kbuf.at[b, core, zc], kbuf.at[b, core, zc], k2_sem.at[b, d], z_peer[d]) for d in range(3)])
        for copy in v1[b]:
            copy.wait_recv()
        v2.append([remote(vbuf.at[b, core, :, yc], vbuf.at[b, core, :, yc], v2_sem.at[b, d], y_peer[d]) for d in range(3)])
        forward_k(b, zc, 3)
        forward_v(b, yc, 3)

    def swap(b):
        for d in (0, 2, 1):
            k2[b][d].wait_recv()
            forward_k(b, (zc + 3 - d) % 4, d)
            v2[b][d].wait_recv()
            forward_v(b, (yc + 3 - d) % 4, d)

    stores, mixes, shared = [], [], []
    channels = qd.shape[2]

    def decode_first(b):
        q_item = qd[b]
        for copy in k3[b]:
            copy.wait_recv()
        keys = kbuf[b].astype(F32).reshape(latents, channels).astype(BF16)
        probs = softmax(dot_t(q_item, keys) * channels**-0.5)
        for copy in v3[b]:
            copy.wait_recv()
        values = vbuf[b].astype(F32).reshape(latents, channels).astype(BF16)
        context = dot(probs, values).astype(BF16)
        mixes.append((q_item.astype(F32) + dot(context, dwo[...])).astype(BF16))

    def decode_last(b):
        mixed = mixes[b]
        hidden = gelu(dot(norm_rows(mixed.astype(F32), gd[...]), dup[...])).astype(BF16)
        x2[b] = (mixed.astype(F32) + dot(hidden, ddn[...])).astype(BF16)
        dst = x2_hbm.at[pl.ds(pl.multiple_of(latents * b + core * mine, mine), mine)]
        shared.append(remote(x2.at[b], dst, share_sem.at[b], partner))
        store = pltpu.make_async_copy(x2.at[b], dst, out_sem.at[b])
        store.start()
        stores.append(store)

    swap(0)
    for b in range(items):
        decode_first(b)
        if b + 1 < items:
            swap(b + 1)
        decode_last(b)

    for copy in shared:
        copy.wait_recv()
    for copy in shared + pair + [swap_r] + sum(sent1 + sent2 + k1 + v1 + k2 + v2 + k3 + v3, []):
        copy.wait_send()
    for store in stores:
        store.wait()


def front(latents, queries, lat_ws, dec_ws, gains):
    items, lat_rows, width = latents.shape
    channels = queries.shape[2]
    head = lat_ws[0].shape[0]
    anywhere = pl.BlockSpec(memory_space=pl.ANY)
    total = items * lat_rows
    dma = pltpu.SemaphoreType.DMA
    return pl.pallas_call(
        front_kernel,
        out_shape=jax.ShapeDtypeStruct((total, channels), BF16),
        in_specs=[anywhere] * 19,
        out_specs=anywhere,
        scratch_shapes=[
            pltpu.VMEM((items, lat_rows, width), BF16),
            pltpu.VMEM((2, items, 8, width), BF16),
            pltpu.VMEM((3, head, width), BF16),
            pltpu.VMEM((head, width), BF16),
            pltpu.VMEM((2, 2, head, width), BF16),
            pltpu.VMEM((items, 8, width), BF16),
            pltpu.VMEM((items, 8, width), BF16),
            pltpu.VMEM((items, lat_rows // 2, channels), BF16),
            pltpu.VMEM((channels, channels), BF16),
            pltpu.VMEM((width, channels), BF16),
            pltpu.VMEM((width, channels), BF16),
            pltpu.VMEM((channels, channels), BF16),
            pltpu.VMEM((channels, channels), BF16),
            pltpu.VMEM((channels, channels), BF16),
            pltpu.VMEM((width,), F32),
            pltpu.VMEM((width,), F32),
            pltpu.VMEM((channels,), F32),
            pltpu.VMEM((width,), F32),
            pltpu.VMEM((channels,), F32),
            pltpu.VMEM((total, width), BF16),
            pltpu.VMEM((total, head), BF16),
            pltpu.VMEM((total, head), BF16),
            pltpu.VMEM((items, 4, 8, width), BF16),
            pltpu.VMEM((items, 4, 8, width), BF16),
            pltpu.VMEM((items, 2, 4, 4, 8, channels), BF16),
            pltpu.VMEM((items, 2, 4, 4, 8, channels), BF16),
            pltpu.VMEM((items, lat_rows // 2, channels), BF16),
            pltpu.VMEM((items, lat_rows // 2, channels), BF16),
            dma((23,)),
            dma((items,)),
            dma((items + 1, 2)),
            dma((2, items, 3, 2)),
            dma((items, 3, 2)),
            dma((items, 3, 2)),
            dma((items, 3, 2)),
            dma((items, 3, 2)),
            dma((items, 4, 2)),
            dma((items, 4, 2)),
            dma((items, 2)),
        ],
        compiler_params=pltpu.CompilerParams(collective_id=0, has_side_effects=True, vmem_limit_bytes=VMEM_BYTES),
        name="front",
    )(latents, queries, *lat_ws, *dec_ws, *gains)


def out_kernel(plan, x2_hbm, wt_hbm, out_hbm, x2, wt, out, x2_sem, wt_sem, out_sem):
    head, (reps, tile), tail = plan
    starts = [sum(head[:t]) for t in range(len(head))]
    base = sum(head)
    ends = [base + reps * tile + sum(tail[:t]) for t in range(len(tail))]
    fixed = list(zip(starts, head)), list(zip(ends, tail))
    steps = len(head) + reps + len(tail)

    def place(i):
        if isinstance(i, int):
            if i < len(head):
                return fixed[0][i]
            if i >= len(head) + reps:
                return fixed[1][i - len(head) - reps]
        return base + (i - len(head)) * tile, tile

    def fetch(i):
        at, width = place(i)
        at = pl.multiple_of(at, 128)
        return pltpu.make_async_copy(wt_hbm.at[:, pl.ds(at, width)], wt.at[i % 2, :, :width], wt_sem.at[i % 2])

    def store(i):
        at, width = place(i)
        at = pl.multiple_of(at, 128)
        return pltpu.make_async_copy(out.at[i % 2, :, :width], out_hbm.at[:, pl.ds(at, width)], out_sem.at[i % 2])

    def product(i):
        width = place(i)[1]
        for at in range(0, x2.shape[0], 384):
            out[i % 2, at : at + 384, :width] = dot(x2[at : at + 384, :], wt[i % 2, :, :width]).astype(BF16)

    def one(i):
        if i + 1 < steps:
            fetch(i + 1).start()
        fetch(i).wait()
        if i >= 2:
            store(i - 2).wait()
        product(i)
        store(i).start()

    load_x2 = pltpu.make_async_copy(x2_hbm, x2, x2_sem)
    load_x2.start()
    fetch(0).start()
    load_x2.wait()
    for i in range(len(head)):
        one(i)
    lo, hi = len(head), len(head) + reps

    def step(i, carry):
        @pl.when(i + 1 < hi)
        def _():
            fetch(i + 1).start()

        @pl.when(i + 1 == hi)
        def _():
            fetch(hi).start()

        fetch(i).wait()
        for t in (lo, lo + 1):
            @pl.when(i == t)
            def _(t=t):
                store(t - 2).wait()

        @pl.when(i >= lo + 2)
        def _():
            store(i - 2).wait()

        product(i)
        store(i).start()
        return carry

    lax.fori_loop(lo, hi, step, 0)
    for i in range(hi, steps):
        one(i)
    store(steps - 2).wait()
    store(steps - 1).wait()


def out_product(x2, dec_out):
    rows, channels = x2.shape
    cols = dec_out.shape[1]
    tile = 4096
    head, tail = (1280, 3072), (2048, 1024)
    plan = (head, ((cols - sum(head) - sum(tail)) // tile, tile), tail)
    anywhere = pl.BlockSpec(memory_space=pl.ANY)
    dma = pltpu.SemaphoreType.DMA
    return pl.pallas_call(
        functools.partial(out_kernel, plan),
        in_specs=[anywhere, anywhere],
        out_specs=anywhere,
        out_shape=jax.ShapeDtypeStruct((rows, cols), BF16),
        scratch_shapes=[
            pltpu.VMEM((rows, channels), BF16),
            pltpu.VMEM((2, channels, tile), BF16),
            pltpu.VMEM((2, rows, tile), BF16),
            dma,
            dma((2,)),
            dma((2,)),
        ],
        compiler_params=pltpu.CompilerParams(vmem_limit_bytes=VMEM_BYTES),
        name="out_product",
    )(x2, dec_out)


def solution(mesh):
    head_split = P(None, "tp", None)
    whole_vec = P(None)
    whole_mat = P(None, None)
    in_specs = (P("dp", None, None), P("dp", "sp", None), whole_vec, head_split, head_split, head_split, P("tp", None, None), whole_vec, P(None, "tp"), P("tp", None), whole_vec, whole_vec, whole_mat, whole_mat, whole_mat, whole_mat, whole_vec, whole_mat, whole_mat, whole_mat)

    def local_step(latents, queries, lat_ln1, lat_wq, lat_wk, lat_wv, lat_wo, lat_ln2, lat_up, lat_down, dec_lnq, dec_lnkv, dec_wq, dec_wk, dec_wv, dec_wo, dec_ln, dec_up, dec_down, dec_out):
        lat_ws = [wt[:, 0, :].T for wt in (lat_wq, lat_wk, lat_wv)] + [lat_wo[0], lat_up.T, lat_down]
        gains = [lat_ln1, lat_ln2, dec_lnq, dec_lnkv, dec_ln]
        x2 = front(latents, queries, lat_ws, [dec_wq, dec_wk, dec_wv, dec_wo, dec_up, dec_down], gains)
        out = out_product(x2, dec_out)
        return out.reshape(queries.shape[0], queries.shape[1], dec_out.shape[1])

    return jax.shard_map(local_step, mesh=mesh, in_specs=in_specs, out_specs=P("dp", "sp", None), check_vma=False)
```

time: 92.2 us -> 84 us (0.911)
  Pallas kernels: 92.1 us -> 83.5 us
    pallas_call x1, Pallas kernels: 46.5 us -> 40.1 us  [front(): pl.pallas_call(front_kernel, out_shape=jax.ShapeDtypeStruct((total, chann...]
    pallas_call x1, Pallas kernels: 45.5 us -> 43.5 us  [out_product(): pl.pallas_call(functools.partial(out_kernel, plan), in_specs=[anywhere, a...]
where the time goes in v4:
time: 84 us; the launch traced here: 83.7 us
  Pallas kernels  83.5 us (99%)
    pallas_call x1, Pallas kernels, out_product(): pl.pallas_call(functools.partial(out_kernel, plan), in_specs=[anywhere, a...  43.5 us
    pallas_call x1, Pallas kernels, front(): pl.pallas_call(front_kernel, out_shape=jax.ShapeDtypeStruct((total, chann...  40.1 us

profile of v4, /device:TPU:1, one launch (start us, length us, event | category | flops | bytes accessed | tf_op | source)
XLA Modules:
  0.0 83.7 jit_solution(13520881895077832910)
XLA Ops:
  0.0 40.1 %front.1.x2_hbm = bf16[768,768]{1,0:T(8,128)(2,1)} custom-call(bf16[3,256,1280]{2,1,0:T(8,128)(2,1)} %z_hbm.1, bf16[3,256,768]{2,1,0:T(8,128)(2,1)} %q_hbm.1, bf16[160,1280]{1,0:T(8,128)(2,1)} %bitcast.12, bf16[160,1280]{1,0:T(8,128)(2,1)} %bitcast.13, bf16[160,1280]{1,0:T(8,128)(2,1)} %bitcast.14, bf16[160,1280]{1,0:T(8,128)(2,1)} %bitcast.15, ...), custom_call_target="tpu_custom_call" | custom-call | tf_op jit(solution)/shard_map/front/pallas_call | solution.py:257
  40.1 43.5 %out_product.1 = bf16[768,32000]{1,0:T(8,128)(2,1)} custom-call(bf16[768,768]{1,0:T(8,128)(2,1)} %front.1.x2_hbm, bf16[768,32000]{1,0:T(8,128)(2,1)} %wt_hbm.1), custom_call_target="tpu_custom_call" | custom-call | tf_op jit(solution)/shard_map/out_product/pallas_call | solution.py:394

commit v5 on v4

--- a/solution.py
+++ b/solution.py
@@ -12,6 +12,8 @@
 F32 = jnp.float32
 BF16 = jnp.bfloat16
 VMEM_BYTES = 67043328
+FIRST_COLS = 2048
+HANDED = 4600 * 1024
 
 
 def norm_rows(widened, gain_row):
@@ -40,11 +42,11 @@
 
 def front_kernel(
     z_hbm, q_hbm, wq_hbm, wk_hbm, wv_hbm, wo_hbm, up_hbm, down_hbm, dwq_hbm, dwk_hbm, dwv_hbm, dwo_hbm, dup_hbm, ddn_hbm,
-    g1_hbm, g2_hbm, gq_hbm, gkv_hbm, gd_hbm,
-    x2_hbm,
+    g1_hbm, g2_hbm, gq_hbm, gkv_hbm, gd_hbm, wout_hbm,
+    x2, first,
     z, zr, wqkv, wo, wmlp, half, taken, queries, dwq, dwk, dwv, dwo, dup, ddn,
-    g1, g2, gq, gkv, gd, normed, khead, vhead, part1, part2, kbuf, vbuf, qd, x2,
-    load_sem, out_sem, pair_sem, x_sem, k1_sem, v1_sem, k2_sem, v2_sem, k3_sem, v3_sem, share_sem,
+    g1, g2, gq, gkv, gd, normed, khead, vhead, part1, part2, kbuf, vbuf, qd,
+    load_sem, pair_sem, x_sem, k1_sem, v1_sem, k2_sem, v2_sem, k3_sem, v3_sem, share_sem,
 ):
     sp, tp = lax.axis_index("sp"), lax.axis_index("tp")
     zc, yc = sp // 4, sp % 4
@@ -82,9 +84,6 @@
     load_zr = [load(z_hbm.at[:, pl.ds(pl.multiple_of(sp * 16 + at * 8, 8), 8), :], zr.at[i]) for i, at in enumerate((core, 1 - core))]
     load_r = [load(wo_hbm, wo), load(up_hbm, wmlp.at[0, 0]), load(down_hbm, wmlp.at[0, 1])]
     mine = latents // 2
-    load_dq = [load(q_hbm.at[:, pl.ds(pl.multiple_of(core * mine, mine), mine), :], queries), load(dwq_hbm, dwq)]
-    load_kv = [load(dwk_hbm, dwk), load(dwv_hbm, dwv)]
-    load_dec = [load(dwo_hbm, dwo), load(dup_hbm, dup), load(ddn_hbm, ddn)]
 
     def norm_item(b):
         for at in range(0, latents, 32):
@@ -120,6 +119,10 @@
     norm_item(0)
     for copy in load_q + load_z[1:] + load_zr + load_r[:1]:
         copy.wait()
+    load_dq = [load(q_hbm.at[:, pl.ds(pl.multiple_of(core * mine, mine), mine), :], queries), load(dwq_hbm, dwq)]
+    load_kv = [load(dwk_hbm, dwk), load(dwv_hbm, dwv)]
+    load_dec = [load(dwo_hbm, dwo), load(dup_hbm, dup), load(ddn_hbm, ddn)]
+    load_first = load(wout_hbm.at[:, : first.shape[1]], first)
     project(0)
     norm_item(1)
     parts = [attend(0)]
@@ -207,7 +210,7 @@
             v2[b][d].wait_recv()
             forward_v(b, (yc + 3 - d) % 4, d)
 
-    stores, mixes, shared = [], [], []
+    mixes, shared = [], []
     channels = qd.shape[2]
 
     def decode_first(b):
@@ -225,12 +228,9 @@
     def decode_last(b):
         mixed = mixes[b]
         hidden = gelu(dot(norm_rows(mixed.astype(F32), gd[...]), dup[...])).astype(BF16)
-        x2[b] = (mixed.astype(F32) + dot(hidden, ddn[...])).astype(BF16)
-        dst = x2_hbm.at[pl.ds(pl.multiple_of(latents * b + core * mine, mine), mine)]
-        shared.append(remote(x2.at[b], dst, share_sem.at[b], partner))
-        store = pltpu.make_async_copy(x2.at[b], dst, out_sem.at[b])
-        store.start()
-        stores.append(store)
+        rows = pl.ds(pl.multiple_of(latents * b + core * mine, mine), mine)
+        x2[rows, :] = (mixed.astype(F32) + dot(hidden, ddn[...])).astype(BF16)
+        shared.append(remote(x2.at[rows], x2.at[rows], share_sem.at[b], partner))
 
     swap(0)
     for b in range(items):
@@ -243,11 +243,10 @@
         copy.wait_recv()
     for copy in shared + pair + [swap_r] + sum(sent1 + sent2 + k1 + v1 + k2 + v2 + k3 + v3, []):
         copy.wait_send()
-    for store in stores:
-        store.wait()
-
-
-def front(latents, queries, lat_ws, dec_ws, gains):
+    load_first.wait()
+
+
+def front(latents, queries, lat_ws, dec_ws, gains, dec_out):
     items, lat_rows, width = latents.shape
     channels = queries.shape[2]
     head = lat_ws[0].shape[0]
@@ -256,9 +255,9 @@
     dma = pltpu.SemaphoreType.DMA
     return pl.pallas_call(
         front_kernel,
-        out_shape=jax.ShapeDtypeStruct((total, channels), BF16),
-        in_specs=[anywhere] * 19,
-        out_specs=anywhere,
+        out_shape=[pltpu.VMEM((total, channels), BF16), pltpu.VMEM((channels, FIRST_COLS), BF16)],
+        in_specs=[anywhere] * 20,
+        out_specs=[pl.BlockSpec(memory_space=pltpu.VMEM)] * 2,
         scratch_shapes=[
             pltpu.VMEM((items, lat_rows, width), BF16),
             pltpu.VMEM((2, items, 8, width), BF16),
@@ -287,9 +286,7 @@
             pltpu.VMEM((items, 2, 4, 4, 8, channels), BF16),
             pltpu.VMEM((items, 2, 4, 4, 8, channels), BF16),
             pltpu.VMEM((items, lat_rows // 2, channels), BF16),
-            pltpu.VMEM((items, lat_rows // 2, channels), BF16),
-            dma((23,)),
-            dma((items,)),
+            dma((24,)),
             dma((items + 1, 2)),
             dma((2, items, 3, 2)),
             dma((items, 3, 2)),
@@ -300,12 +297,12 @@
             dma((items, 4, 2)),
             dma((items, 2)),
         ],
-        compiler_params=pltpu.CompilerParams(collective_id=0, has_side_effects=True, vmem_limit_bytes=VMEM_BYTES),
+        compiler_params=pltpu.CompilerParams(collective_id=0, has_side_effects=True, vmem_limit_bytes=VMEM_BYTES - HANDED),
         name="front",
-    )(latents, queries, *lat_ws, *dec_ws, *gains)
-
-
-def out_kernel(plan, x2_hbm, wt_hbm, out_hbm, x2, wt, out, x2_sem, wt_sem, out_sem):
+    )(latents, queries, *lat_ws, *dec_ws, *gains, dec_out)
+
+
+def out_kernel(plan, x2, first, wt_hbm, out_hbm, wt, out, wt_sem, out_sem):
     head, (reps, tile), tail = plan
     starts = [sum(head[:t]) for t in range(len(head))]
     base = sum(head)
@@ -334,21 +331,19 @@
     def product(i):
         width = place(i)[1]
         for at in range(0, x2.shape[0], 384):
-            out[i % 2, at : at + 384, :width] = dot(x2[at : at + 384, :], wt[i % 2, :, :width]).astype(BF16)
+            weights = first[...] if isinstance(i, int) and i == 0 else wt[i % 2, :, :width]
+            out[i % 2, at : at + 384, :width] = dot(x2[at : at + 384, :], weights).astype(BF16)
 
     def one(i):
         if i + 1 < steps:
             fetch(i + 1).start()
-        fetch(i).wait()
+        if i:
+            fetch(i).wait()
         if i >= 2:
             store(i - 2).wait()
         product(i)
         store(i).start()
 
-    load_x2 = pltpu.make_async_copy(x2_hbm, x2, x2_sem)
-    load_x2.start()
-    fetch(0).start()
-    load_x2.wait()
     for i in range(len(head)):
         one(i)
     lo, hi = len(head), len(head) + reps
@@ -383,30 +378,28 @@
     store(steps - 1).wait()
 
 
-def out_product(x2, dec_out):
+def out_product(x2, first, dec_out):
     rows, channels = x2.shape
     cols = dec_out.shape[1]
     tile = 4096
-    head, tail = (1280, 3072), (2048, 1024)
+    head, tail = (FIRST_COLS, 3072), (1280, 1024)
     plan = (head, ((cols - sum(head) - sum(tail)) // tile, tile), tail)
     anywhere = pl.BlockSpec(memory_space=pl.ANY)
     dma = pltpu.SemaphoreType.DMA
     return pl.pallas_call(
         functools.partial(out_kernel, plan),
-        in_specs=[anywhere, anywhere],
+        in_specs=[pl.BlockSpec(memory_space=pltpu.VMEM)] * 2 + [anywhere],
         out_specs=anywhere,
         out_shape=jax.ShapeDtypeStruct((rows, cols), BF16),
         scratch_shapes=[
-            pltpu.VMEM((rows, channels), BF16),
             pltpu.VMEM((2, channels, tile), BF16),
             pltpu.VMEM((2, rows, tile), BF16),
-            dma,
             dma((2,)),
             dma((2,)),
         ],
-        compiler_params=pltpu.CompilerParams(vmem_limit_bytes=VMEM_BYTES),
+        compiler_params=pltpu.CompilerParams(vmem_limit_bytes=40 * 2**20),
         name="out_product",
-    )(x2, dec_out)
+    )(x2, first, dec_out)
 
 
 def solution(mesh):
@@ -418,8 +411,8 @@
     def local_step(latents, queries, lat_ln1, lat_wq, lat_wk, lat_wv, lat_wo, lat_ln2, lat_up, lat_down, dec_lnq, dec_lnkv, dec_wq, dec_wk, dec_wv, dec_wo, dec_ln, dec_up, dec_down, dec_out):
         lat_ws = [wt[:, 0, :].T for wt in (lat_wq, lat_wk, lat_wv)] + [lat_wo[0], lat_up.T, lat_down]
         gains = [lat_ln1, lat_ln2, dec_lnq, dec_lnkv, dec_ln]
-        x2 = front(latents, queries, lat_ws, [dec_wq, dec_wk, dec_wv, dec_wo, dec_up, dec_down], gains)
-        out = out_product(x2, dec_out)
+        x2, first = front(latents, queries, lat_ws, [dec_wq, dec_wk, dec_wv, dec_wo, dec_up, dec_down], gains, dec_out)
+        out = out_product(x2, first, dec_out)
         return out.reshape(queries.shape[0], queries.shape[1], dec_out.shape[1])
 
     return jax.shard_map(local_step, mesh=mesh, in_specs=in_specs, out_specs=P("dp", "sp", None), check_vma=False)

time: 84 us -> 83.3 us (level)
  no operation moved by 1% of the time
where the time goes in v5:
time: 83.3 us; the launch traced here: 83.2 us
  Pallas kernels  83 us (100%)
    pallas_call x1, Pallas kernels, out_product(): pl.pallas_call(functools.partial(out_kernel, plan), in_specs=[pl.BlockSpe...  43 us
    pallas_call x1, Pallas kernels, front(): pl.pallas_call(front_kernel, out_shape=[pltpu.VMEM((total, channels), BF1...  40 us

profile of v5, /device:TPU:1, one launch (start us, length us, event | category | flops | bytes accessed | tf_op | source)
XLA Modules:
  0.0 83.2 jit_solution(18428123072943843428)
XLA Ops:
  0.0 40.0 %front.1 = (bf16[768,768]{1,0:T(8,128)(2,1)S(1)}, bf16[768,2048]{1,0:T(8,128)(2,1)S(1)}) custom-call(bf16[3,256,1280]{2,1,0:T(8,128)(2,1)} %z_hbm.1, bf16[3,256,768]{2,1,0:T(8,128)(2,1)} %q_hbm.1, bf16[160,1280]{1,0:T(8,128)(2,1)} %bitcast.12, bf16[160,1280]{1,0:T(8,128)(2,1)} %bitcast.13, bf16[160,1280]{1,0:T(8,128)(2,1)} %bitcast.14, ...), custom_call_target="tpu_custom_call" | custom-call | tf_op jit(solution)/shard_map/front/pallas_call | solution.py:256
  40.0 43.0 %out_product.1 = bf16[768,32000]{1,0:T(8,128)(2,1)} custom-call(bf16[768,768]{1,0:T(8,128)(2,1)S(1)} %get-tuple-element.7.x2, bf16[768,2048]{1,0:T(8,128)(2,1)S(1)} %get-tuple-element.8.first, bf16[768,32000]{1,0:T(8,128)(2,1)} %wt_hbm.1), custom_call_target="tpu_custom_call" | custom-call | tf_op jit(solution)/shard_map/out_product/pallas_call | solution.py:389

commit v6 on v5

--- a/solution.py
+++ b/solution.py
@@ -44,7 +44,7 @@
     z_hbm, q_hbm, wq_hbm, wk_hbm, wv_hbm, wo_hbm, up_hbm, down_hbm, dwq_hbm, dwk_hbm, dwv_hbm, dwo_hbm, dup_hbm, ddn_hbm,
     g1_hbm, g2_hbm, gq_hbm, gkv_hbm, gd_hbm, wout_hbm,
     x2, first,
-    z, zr, wqkv, wo, wmlp, half, taken, queries, dwq, dwk, dwv, dwo, dup, ddn,
+    z, zr, wqkv, wo, wmlp, half, taken, queries, dwq, dwkv, dwo, dup, ddn,
     g1, g2, gq, gkv, gd, normed, khead, vhead, part1, part2, kbuf, vbuf, qd,
     load_sem, pair_sem, x_sem, k1_sem, v1_sem, k2_sem, v2_sem, k3_sem, v3_sem, share_sem,
 ):
@@ -97,8 +97,7 @@
         vhead[latents * b : latents * (b + 1), :] = dot_t(item(normed, b), wqkv[2]).astype(BF16)
 
     def attend(b):
-        chip_rows = jnp.concatenate([zr[0, b].astype(F32), zr[1, b].astype(F32)], axis=0)
-        q_rows = dot_t(norm_rows(chip_rows, g1[...]), wqkv[0]).astype(BF16)
+        q_rows = q_all[16 * b : 16 * (b + 1)].astype(BF16)
         probs = softmax(dot_t(q_rows, item(khead, b)) * q_rows.shape[1] ** -0.5)
         context = dot(probs, item(vhead, b)).astype(BF16)
         return dot(context, wo[...])
@@ -120,9 +119,12 @@
     for copy in load_q + load_z[1:] + load_zr + load_r[:1]:
         copy.wait()
     load_dq = [load(q_hbm.at[:, pl.ds(pl.multiple_of(core * mine, mine), mine), :], queries), load(dwq_hbm, dwq)]
-    load_kv = [load(dwk_hbm, dwk), load(dwv_hbm, dwv)]
+    chans = q_hbm.shape[2]
+    load_kv = [load(dwk_hbm, dwkv.at[:, :chans]), load(dwv_hbm, dwkv.at[:, chans:])]
     load_dec = [load(dwo_hbm, dwo), load(dup_hbm, dup), load(ddn_hbm, ddn)]
     load_first = load(wout_hbm.at[:, : first.shape[1]], first)
+    chip_rows = jnp.concatenate([zr[i, b].astype(F32) for b in range(items) for i in range(2)], axis=0)
+    q_all = dot_t(norm_rows(chip_rows, g1[...]), wqkv[0])
     project(0)
     norm_item(1)
     parts = [attend(0)]
@@ -133,13 +135,13 @@
     parts.append(attend(1))
     project(2)
     give(1, parts[1])
+    spread(0, parts[0])
     parts.append(attend(2))
-    spread(0, parts[0])
     give(2, parts[2])
+    spread(1, parts[1])
     for copy in load_r[1:]:
         copy.wait()
     swap_r = remote(wmlp.at[0], wmlp.at[1], pair_sem.at[items], partner)
-    spread(1, parts[1])
     spread(2, parts[2])
 
     for copy in load_dq:
@@ -176,8 +178,9 @@
             copy.wait_recv()
         z_new = (z_mid[b].astype(F32) + gather_sum(part2, b)).astype(BF16)
         kv_in = norm_rows(z_new.astype(F32), gkv[...])
-        kbuf[b, core, zc, yc] = dot(kv_in, dwk[...]).astype(BF16)
-        vbuf[b, core, zc, yc] = dot(kv_in, dwv[...]).astype(BF16)
+        both = dot(kv_in, dwkv[...])
+        kbuf[b, core, zc, yc] = both[:, :chans].astype(BF16)
+        vbuf[b, core, zc, yc] = both[:, chans:].astype(BF16)
         k1.append([remote(kbuf.at[b, core, zc, yc], kbuf.at[b, core, zc, yc], k1_sem.at[b, d], y_peer[d]) for d in range(3)])
         v1.append([remote(vbuf.at[b, core, zc, yc], vbuf.at[b, core, zc, yc], v1_sem.at[b, d], z_peer[d]) for d in range(3)])
 
@@ -268,8 +271,7 @@
             pltpu.VMEM((items, 8, width), BF16),
             pltpu.VMEM((items, lat_rows // 2, channels), BF16),
             pltpu.VMEM((channels, channels), BF16),
-            pltpu.VMEM((width, channels), BF16),
-            pltpu.VMEM((width, channels), BF16),
+            pltpu.VMEM((width, 2 * channels), BF16),
             pltpu.VMEM((channels, channels), BF16),
             pltpu.VMEM((channels, channels), BF16),
             pltpu.VMEM((channels, channels), BF16),
@@ -382,7 +384,7 @@
     rows, channels = x2.shape
     cols = dec_out.shape[1]
     tile = 4096
-    head, tail = (FIRST_COLS, 3072), (1280, 1024)
+    head, tail = (FIRST_COLS, 3072), (1792, 512)
     plan = (head, ((cols - sum(head) - sum(tail)) // tile, tile), tail)
     anywhere = pl.BlockSpec(memory_space=pl.ANY)
     dma = pltpu.SemaphoreType.DMA

time: 83.3 us -> 81.6 us (0.980)
  Pallas kernels: 83 us -> 81.4 us
    pallas_call x1, Pallas kernels: 43 us -> 42.1 us  [out_product(): pl.pallas_call(functools.partial(out_kernel, plan), in_specs=[pl.BlockSpe...]
where the time goes in v6:
time: 81.6 us; the launch traced here: 81.5 us
  Pallas kernels  81.4 us (100%)
    pallas_call x1, Pallas kernels, out_product(): pl.pallas_call(functools.partial(out_kernel, plan), in_specs=[pl.BlockSpe...  42.1 us
    pallas_call x1, Pallas kernels, front(): pl.pallas_call(front_kernel, out_shape=[pltpu.VMEM((total, channels), BF1...  39.2 us

profile of v6, /device:TPU:1, one launch (start us, length us, event | category | flops | bytes accessed | tf_op | source)
XLA Modules:
  0.0 81.5 jit_solution(17487191470935623985)
XLA Ops:
  0.0 39.2 %front.1 = (bf16[768,768]{1,0:T(8,128)(2,1)S(1)}, bf16[768,2048]{1,0:T(8,128)(2,1)S(1)}) custom-call(bf16[3,256,1280]{2,1,0:T(8,128)(2,1)} %z_hbm.1, bf16[3,256,768]{2,1,0:T(8,128)(2,1)} %q_hbm.1, bf16[160,1280]{1,0:T(8,128)(2,1)} %bitcast.12, bf16[160,1280]{1,0:T(8,128)(2,1)} %bitcast.13, bf16[160,1280]{1,0:T(8,128)(2,1)} %bitcast.14, ...), custom_call_target="tpu_custom_call" | custom-call | tf_op jit(solution)/shard_map/front/pallas_call | solution.py:259
  39.2 42.1 %out_product.1 = bf16[768,32000]{1,0:T(8,128)(2,1)} custom-call(bf16[768,768]{1,0:T(8,128)(2,1)S(1)} %get-tuple-element.7.x2, bf16[768,2048]{1,0:T(8,128)(2,1)S(1)} %get-tuple-element.8.first, bf16[768,32000]{1,0:T(8,128)(2,1)} %wt_hbm.1), custom_call_target="tpu_custom_call" | custom-call | tf_op jit(solution)/shard_map/out_product/pallas_call | solution.py:391
